TPU v7x, 8 devices: a whole 2x2x1 slice. The times are simulated.
8 devices in a mesh: dp: 2 (over z, y), ep: 4 (over x, core).
Axes of the slice: x: 2, y: 2, z: 1, core: 2. Of those that a mesh axis runs over, the one named last changes fastest.
Arguments:
- x_in: bfloat16 [4096, 512], P(('dp', 'ep')), parts along dimension 0
- idx_a: int32 [4096, 2], P(('dp', 'ep')), parts along dimension 0
- idx_b: int32 [4096, 2], P(('dp', 'ep')), parts along dimension 0
- gate_a: float32 [4096, 2], P(('dp', 'ep')), parts along dimension 0
- gate_b: float32 [4096, 2], P(('dp', 'ep')), parts along dimension 0
- dy_out: bfloat16 [4096, 512], P(('dp', 'ep')), parts along dimension 0
- w1_a: bfloat16 [8, 512, 1792], P('ep')
- w3_a: bfloat16 [8, 512, 1792], P('ep')
- w2_a: bfloat16 [8, 1792, 512], P('ep')
- w1_b: bfloat16 [8, 512, 1792], P('ep')
- w3_b: bfloat16 [8, 512, 1792], P('ep')
- w2_b: bfloat16 [8, 1792, 512], P('ep')
Outputs:
- output 1: bfloat16 [4096, 512], P(('dp', 'ep')), parts along dimension 0
- output 2: bfloat16 [4096, 512], P(('dp', 'ep')), parts along dimension 0
- output 3: float32 [16, 512, 1792], P(('dp', 'ep')), parts along dimension 0
- output 4: float32 [16, 512, 1792], P(('dp', 'ep')), parts along dimension 0
- output 5: float32 [16, 1792, 512], P(('dp', 'ep')), parts along dimension 0
- output 6: float32 [16, 512, 1792], P(('dp', 'ep')), parts along dimension 0
- output 7: float32 [16, 512, 1792], P(('dp', 'ep')), parts along dimension 0
- output 8: float32 [16, 1792, 512], P(('dp', 'ep')), parts along dimension 0
- output 9: float32 [4096, 2], P(('dp', 'ep')), parts along dimension 0
- output 10: float32 [4096, 2], P(('dp', 'ep')), parts along dimension 0
There are 2 independent parts. A program takes and returns all parts, laid end to end along the dimension named above; an argument that names none is the same for every part.
All inputs are finite; a program needn't handle non-finite values.
Results may differ from a plain program's by a relative error of at most 0.00787.
Values are sent between devices in bfloat16 or wider.
A program may use at most 1 GiB of HBM per device.

v0:
```python
import jax
import jax.numpy as jnp
from jax import lax
from jax.sharding import PartitionSpec as P

CAP_FACTOR = 4


def slot_maps(dev_ids, experts, capacity):
    pair_total = dev_ids.shape[0] * dev_ids.shape[1]
    flat_ids = dev_ids.reshape(-1)
    onehot = (flat_ids[:, None] == jnp.arange(experts, dtype=jnp.int32)[None, :]).astype(jnp.int32)
    pair_slot = jnp.sum(jnp.cumsum(onehot, axis=0) * onehot, axis=1) - 1
    pair_row = flat_ids * capacity + pair_slot
    pair_ids = jnp.arange(pair_total, dtype=jnp.int32)
    row_pair = jnp.full((experts * capacity,), pair_total, jnp.int32).at[pair_row].set(pair_ids)
    return pair_row, row_pair


def send_rows(rows, index, capacity):
    send_buf = jnp.take(rows, index, axis=0, mode="fill", fill_value=0)
    send_buf = send_buf.reshape((index.shape[0] // capacity, capacity) + send_buf.shape[1:])
    return lax.all_to_all(send_buf, "ep", 0, 1, tiled=True)


def send_back(rows):
    back_rows = lax.all_to_all(rows, "ep", 1, 0, tiled=True)
    return back_rows.reshape((back_rows.shape[0] * back_rows.shape[1],) + back_rows.shape[2:])


def expert_forward(u_rows, w_gate, w_up, w_down):
    pre_gate = jnp.einsum("erd,edf->erf", u_rows, w_gate, preferred_element_type=jnp.float32)
    pre_up = jnp.einsum("erd,edf->erf", u_rows, w_up, preferred_element_type=jnp.float32)
    hidden = (jax.nn.silu(pre_gate) * pre_up).astype(jnp.bfloat16)
    out_rows = jnp.einsum("erf,efd->erd", hidden, w_down, preferred_element_type=jnp.float32).astype(jnp.bfloat16)
    return pre_gate, pre_up, hidden, out_rows


def expert_backward(u_rows, dy_rows, gate_rows, w_gate, w_up, w_down):
    pre_gate, pre_up, hidden, out_rows = expert_forward(u_rows, w_gate, w_up, w_down)
    dgate_rows = jnp.einsum("erd,erd->er", dy_rows, out_rows, preferred_element_type=jnp.float32)
    d_out = (gate_rows[:, :, None] * dy_rows).astype(jnp.bfloat16)
    dw_down = jnp.einsum("erf,erd->efd", hidden, d_out, preferred_element_type=jnp.float32)
    d_hidden = jnp.einsum("erd,efd->erf", d_out, w_down, preferred_element_type=jnp.float32)
    gate_sig = jax.nn.sigmoid(pre_gate)
    d_pre_gate = (d_hidden * pre_up * gate_sig * (1.0 + pre_gate * (1.0 - gate_sig))).astype(jnp.bfloat16)
    d_pre_up = (d_hidden * jax.nn.silu(pre_gate)).astype(jnp.bfloat16)
    dw_gate = jnp.einsum("erd,erf->edf", u_rows, d_pre_gate, preferred_element_type=jnp.float32)
    dw_up = jnp.einsum("erd,erf->edf", u_rows, d_pre_up, preferred_element_type=jnp.float32)
    du_rows = (jnp.einsum("erf,edf->erd", d_pre_gate, w_gate, preferred_element_type=jnp.float32) + jnp.einsum("erf,edf->erd", d_pre_up, w_up, preferred_element_type=jnp.float32)).astype(jnp.bfloat16)
    return du_rows, dgate_rows, dw_gate, dw_up, dw_down


def combine(x_rows, gates, back_rows, pair_row):
    tok_dev, top_k = gates.shape
    out_pairs = jnp.take(back_rows, pair_row, axis=0).reshape(tok_dev, top_k, -1)
    branch = jnp.sum(gates[:, :, None] * out_pairs, axis=1)
    return (x_rows.astype(jnp.float32) + branch).astype(jnp.bfloat16)


def layer_backward(dy_rows, u_rows, gates, row_maps, capacity, w_gate, w_up, w_down):
    pair_row, row_pair = row_maps
    tok_dev, top_k = gates.shape
    dy_sent = send_rows(dy_rows, row_pair // top_k, capacity)
    gate_sent = send_rows(gates.reshape(-1), row_pair, capacity)
    u_rows, dy_sent = lax.optimization_barrier((u_rows, dy_sent))
    du_rows, dgate_rows, dw_gate, dw_up, dw_down = expert_backward(u_rows, dy_sent, gate_sent, w_gate, w_up, w_down)
    du_pairs = jnp.take(send_back(du_rows), pair_row, axis=0).reshape(tok_dev, top_k, -1)
    dx_rows = (dy_rows.astype(jnp.float32) + jnp.sum(du_pairs, axis=1, dtype=jnp.float32)).astype(jnp.bfloat16)
    dgate_out = jnp.take(send_back(dgate_rows), pair_row, axis=0).reshape(tok_dev, top_k)
    return dx_rows, dgate_out, (dw_gate, dw_up, dw_down)


def solution(mesh):
    n_group = mesh.shape["ep"]
    tok_spec = P(("dp", "ep"))
    w_spec = P("ep")

    def device_program(x_in, idx_a, idx_b, gate_a, gate_b, dy_out, w1_a, w3_a, w2_a, w1_b, w3_b, w2_b):
        tok_dev, top_k = idx_a.shape
        experts = w1_a.shape[0] * n_group
        capacity = CAP_FACTOR * tok_dev * top_k // experts
        maps_a = slot_maps(idx_a, experts, capacity)
        maps_b = slot_maps(idx_b, experts, capacity)
        u_rows_a = send_rows(x_in, maps_a[1] // top_k, capacity)
        out_a = expert_forward(u_rows_a, w1_a, w3_a, w2_a)[3]
        x_mid = combine(x_in, gate_a, send_back(out_a), maps_a[0])
        u_rows_b = send_rows(x_mid, maps_b[1] // top_k, capacity)
        out_b = expert_forward(u_rows_b, w1_b, w3_b, w2_b)[3]
        x_out = combine(x_mid, gate_b, send_back(out_b), maps_b[0])
        dx_mid, dgate_b, grads_b = layer_backward(dy_out, u_rows_b, gate_b, maps_b, capacity, w1_b, w3_b, w2_b)
        x_again, dx_mid = lax.optimization_barrier((x_in, dx_mid))
        u_again = send_rows(x_again, maps_a[1] // top_k, capacity)
        dx_in, dgate_a, grads_a = layer_backward(dx_mid, u_again, gate_a, maps_a, capacity, w1_a, w3_a, w2_a)
        return (x_out, dx_in) + grads_a + grads_b + (dgate_a, dgate_b)

    return jax.shard_map(device_program, mesh=mesh, in_specs=(tok_spec,) * 6 + (w_spec,) * 6, out_specs=(tok_spec,) * 10, check_vma=False)
```

profile of v0, /device:TPU:0, one launch (start us, length us, event | category | flops | bytes accessed | tf_op | source)
XLA Modules:
  0.0 1023.7 jit_solution(11956432849156085162)
XLA Ops:
  10.8 17.3 %gather_fusion = bf16[4096,512]{1,0:T(8,128)(2,1)} fusion(bf16[512,512]{1,0:T(8,128)(2,1)S(1)} %copy-done, s32[4096]{0:T(1024)S(1)} %get-tuple-element.55), kind=kCustom, calls=%fused_computation.clone | custom fusion | bytes 8404992 | tf_op jit(solution)/shard_map/jit(_take)/gather | solution.py:21
  30.8 52.7 %all_to_all.214 = bf16[8,512,512]{2,1,0:T(8,128)(2,1)S(1)} all-to-all(bf16[8,512,512]{2,1,0:T(8,128)(2,1)S(1)} %bitcast.147), channel_id=1, replica_groups=mesh['dp'=2,'ep'=4] {'ep'}, dimensions={0} | all-to-all | bytes 8388608 | tf_op jit(solution)/shard_map/all_to_all | solution.py:23
  85.5 13.7 %fusion.37 = f32[2,2048,1792]{2,1,0:T(8,128)} fusion(bf16[2,2048,512]{2,1,0:T(8,128)(2,1)S(1)} %bitcast.160, bf16[2,512,1792]{2,1,0:T(8,128)(2,1)S(1)} %copy-done.49), kind=kOutput, calls=%fused_computation.123 | convolution fusion | flops 7516192768 | bytes 37224448 | tf_op jit(solution)/shard_map/erd,edf->erf/dot_general | solution.py:33
  99.2 13.6 %fusion.36 = f32[2,2048,1792]{2,1,0:T(8,128)} fusion(bf16[2,2048,512]{2,1,0:T(8,128)(2,1)S(1)} %bitcast.161, bf16[2,512,1792]{2,1,0:T(8,128)(2,1)S(1)} %copy-done.45), kind=kOutput, calls=%fused_computation.122 | convolution fusion | flops 7516192768 | bytes 37224448 | tf_op jit(solution)/shard_map/erd,edf->erf/dot_general | solution.py:32
  112.8 23.7 %fusion.9 = bf16[2,2048,512]{2,1,0:T(8,128)(2,1)} fusion(bf16[2,1792,512]{2,1,0:T(8,128)(2,1)} %param.28, f32[2,2048,1792]{2,1,0:T(8,128)} %fusion.37, f32[2,2048,1792]{2,1,0:T(8,128)} %fusion.36), kind=kOutput, calls=%fused_computation.45 | convolution fusion | flops 7562330112 | bytes 66584576 | tf_op jit(solution)/shard_map/erf,efd->erd/dot_general | solution.py:35
  160.7 17.3 %gather_fusion.5 = bf16[4096,512]{1,0:T(8,128)(2,1)} fusion(bf16[512,512]{1,0:T(8,128)(2,1)S(1)} %copy-done.6, s32[4096]{0:T(1024)S(1)} %get-tuple-element.57), kind=kCustom, calls=%fused_computation.5.clone | custom fusion | bytes 8404992 | tf_op jit(solution)/shard_map/jit(_take)/gather | solution.py:21
  178.1 21.6 %all-to-all-done.1 = bf16[2,2048,512]{2,0,1:T(2,128)(2,1)} async-done(((bf16[2,2048,512]{2,0,1:T(2,128)(2,1)}), bf16[2,2048,512]{2,0,1:T(2,128)(2,1)}, u32[]{:S(2)}, u32[]{:S(2)}) %all-to-all-start.1) | async-done | bytes 4194336 | tf_op jit(solution)/shard_map/all_to_all | solution.py:27
  220.8 17.3 %gather_fusion.2 = bf16[4096,512]{1,0:T(8,128)(2,1)} fusion(bf16[512,512]{1,0:T(8,128)(2,1)S(1)} %add_convert_fusion.5, s32[4096]{0:T(1024)S(1)} %get-tuple-element.57), kind=kCustom, calls=%fused_computation.4.clone | custom fusion | bytes 8404992 | tf_op jit(solution)/shard_map/jit(_take)/gather | solution.py:21
  243.4 51.5 %all_to_all.215 = bf16[8,512,512]{2,1,0:T(8,128)(2,1)} all-to-all(bf16[8,512,512]{2,1,0:T(8,128)(2,1)S(1)} %bitcast.143), channel_id=1, replica_groups=mesh['dp'=2,'ep'=4] {'ep'}, dimensions={0} | all-to-all | bytes 8388608 | tf_op jit(solution)/shard_map/all_to_all | solution.py:23
  300.2 16.7 %gather_fusion.4 = f32[4096]{0:T(1024)S(1)} fusion(f32[1024]{0:T(1024)S(1)} %reshape.233, s32[4096]{0:T(1024)S(1)} %get-tuple-element.56), kind=kCustom, calls=%fused_computation.2.clone | custom fusion | bytes 49152 | tf_op jit(solution)/shard_map/jit(_take)/gather | solution.py:21
  322.0 25.7 %all-to-all-done.5 = bf16[8,512,512]{2,1,0:T(8,128)(2,1)} async-done(((bf16[8,512,512]{2,1,0:T(8,128)(2,1)}), bf16[8,512,512]{2,1,0:T(8,128)(2,1)}, u32[]{:S(2)}, u32[]{:S(2)}) %all-to-all-start.5) | async-done | bytes 4194336 | tf_op jit(solution)/shard_map/all_to_all | solution.py:23
  357.5 13.7 %fusion.39 = f32[2,2048,1792]{2,1,0:T(8,128)} fusion(bf16[2,2048,512]{2,1,0:T(8,128)(2,1)S(1)} %bitcast.152, bf16[2,512,1792]{2,1,0:T(8,128)(2,1)S(1)} %copy-done.43), kind=kOutput, calls=%fused_computation.125 | convolution fusion | flops 7516192768 | bytes 37224448 | tf_op jit(solution)/shard_map/erd,edf->erf/dot_general | solution.py:33
  371.1 13.6 %fusion.40 = f32[2,2048,1792]{2,1,0:T(8,128)} fusion(bf16[2,2048,512]{2,1,0:T(8,128)(2,1)S(1)} %bitcast.153, bf16[2,512,1792]{2,1,0:T(8,128)(2,1)S(1)} %copy-done.43), kind=kOutput, calls=%fused_computation.126 | convolution fusion | flops 7516192768 | bytes 37224448 | tf_op jit(solution)/shard_map/erd,edf->erf/dot_general | solution.py:33
  384.8 13.6 %fusion.41 = f32[2,2048,1792]{2,1,0:T(8,128)} fusion(bf16[2,2048,512]{2,1,0:T(8,128)(2,1)S(1)} %bitcast.154, bf16[2,512,1792]{2,1,0:T(8,128)(2,1)S(1)} %copy-done.44), kind=kOutput, calls=%fused_computation.127 | convolution fusion | flops 7516192768 | bytes 37224448 | tf_op jit(solution)/shard_map/erd,edf->erf/dot_general | solution.py:32
  398.4 41.9 %multiply_convert_fusion.4 = (bf16[2,2048,1792]{2,1,0:T(8,128)(2,1)}, bf16[2,2048,1792]{2,1,0:T(8,128)(2,1)}, bf16[2,2048,1792]{2,1,0:T(8,128)(2,1)}) fusion(f32[2,2048,1792]{2,1,0:T(8,128)} %fusion.41, f32[2,2048,1792]{2,1,0:T(8,128)} %fusion.40, bf16[2,1792,512]{2,1,0:T(8,128)(2,1)} %param.31, bf16[2,2048,512]{2,1,0:T(8,128)(2,1)} %bitcast.148, ...), kind=kOutput, calls=%fused_computation.21 | convolution fusion | flops 7632584704 | bytes 110641152 | tf_op jit(solution)/shard_map/erd,efd->erf/dot_general | solution.py:44
  457.0 14.1 %fusion.42 = f32[2,2048,512]{2,1,0:T(8,128)} fusion(bf16[2,2048,1792]{2,1,0:T(8,128)(2,1)} %get-tuple-element.52, bf16[2,512,1792]{2,1,0:T(8,128)(2,1)} %param.29), kind=kOutput, calls=%fused_computation.128 | convolution fusion | flops 7516192768 | bytes 26738688 | tf_op jit(solution)/shard_map/erf,edf->erd/dot_general | solution.py:50
  484.6 15.7 %fusion.38 = f32[2,2048,1792]{2,1,0:T(8,128)} fusion(bf16[2,2048,512]{2,1,0:T(8,128)(2,1)S(1)} %bitcast.155, bf16[2,512,1792]{2,1,0:T(8,128)(2,1)} %param.29), kind=kOutput, calls=%fused_computation.124 | convolution fusion | flops 7516192768 | bytes 37224448 | tf_op jit(solution)/shard_map/erd,edf->erf/dot_general | solution.py:32
  500.3 19.0 %copy.80 = bf16[2,2048,512]{2,0,1:T(2,128)(2,1)} copy(bf16[2,2048,512]{2,1,0:T(8,128)(2,1)S(1)} %add_convert_fusion.1) | data formatting | bytes 8388608 | tf_op jit(solution)/shard_map/convert_element_type | solution.py:50
  524.6 23.8 %fusion.8 = bf16[2,2048,512]{2,1,0:T(8,128)(2,1)} fusion(bf16[2,1792,512]{2,1,0:T(8,128)(2,1)} %param.31, f32[2,2048,1792]{2,1,0:T(8,128)} %fusion.39, f32[2,2048,1792]{2,1,0:T(8,128)} %fusion.38), kind=kOutput, calls=%fused_computation.44 | convolution fusion | flops 7562330112 | bytes 66584576 | tf_op jit(solution)/shard_map/erf,efd->erd/dot_general | solution.py:35
  558.5 14.0 %all-to-all-done.6 = bf16[2,2048,512]{2,0,1:T(2,128)(2,1)} async-done(((bf16[2,2048,512]{2,0,1:T(2,128)(2,1)}), bf16[2,2048,512]{2,0,1:T(2,128)(2,1)}, u32[]{:S(2)}, u32[]{:S(2)}) %all-to-all-start.6) | async-done | bytes 4194336 | tf_op jit(solution)/shard_map/all_to_all | solution.py:27
  577.6 16.7 %gather_fusion.7 = f32[4096]{0:T(1024)S(1)} fusion(f32[1024]{0:T(1024)S(1)} %reshape.236, s32[4096]{0:T(1024)S(1)} %copy-done.29), kind=kCustom, calls=%fused_computation.11.clone | custom fusion | bytes 49152 | tf_op jit(solution)/shard_map/jit(_take)/gather | solution.py:21
  647.5 17.3 %gather_fusion.8 = bf16[4096,512]{1,0:T(8,128)(2,1)} fusion(bf16[512,512]{1,0:T(8,128)(2,1)S(1)} %copy-done.1, s32[4096]{0:T(1024)S(1)} %copy-done.21), kind=kCustom, calls=%fused_computation.6.clone | custom fusion | bytes 8404992 | tf_op jit(solution)/shard_map/jit(_take)/gather | solution.py:21
  664.8 17.3 %gather_fusion.9 = bf16[4096,512]{1,0:T(8,128)(2,1)} fusion(bf16[512,512]{1,0:T(8,128)(2,1)S(1)} %add_convert_fusion.3, s32[4096]{0:T(1024)S(1)} %copy-done.21), kind=kCustom, calls=%fused_computation.7.clone | custom fusion | bytes 8404992 | tf_op jit(solution)/shard_map/jit(_take)/gather | solution.py:21
  693.3 15.9 %fusion.48 = f32[2,512,1792]{2,1,0:T(8,128)} fusion(bf16[2,2048,512]{2,1,0:T(8,128)(2,1)} %bitcast.151, bf16[2,2048,1792]{2,1,0:T(8,128)(2,1)} %get-tuple-element.51), kind=kOutput, calls=%fused_computation.134 | convolution fusion | flops 7516192768 | bytes 26214400 | tf_op jit(solution)/shard_map/erd,erf->edf/dot_general | solution.py:49
  719.4 21.8 %all-to-all-done.8 = bf16[8,512,512]{2,1,0:T(8,128)(2,1)} async-done(((bf16[8,512,512]{2,1,0:T(8,128)(2,1)}), bf16[8,512,512]{2,1,0:T(8,128)(2,1)}, u32[]{:S(2)}, u32[]{:S(2)}) %all-to-all-start.8) | async-done | bytes 4194336 | tf_op jit(solution)/shard_map/all_to_all | solution.py:23
  746.4 14.8 %fusion.14 = f32[2,1792,512]{2,1,0:T(8,128)} fusion(bf16[2,2048,1792]{2,1,0:T(8,128)(2,1)} %get-tuple-element.53, bf16[2,2048,512]{2,1,0:T(8,128)(2,1)} %bitcast.150, f32[2,2048]{1,0:T(2,128)S(1)} %bitcast.167), kind=kOutput, calls=%fused_computation.48 | convolution fusion | flops 7522484224 | bytes 26230784 | tf_op jit(solution)/shard_map/erf,erd->efd/dot_general | solution.py:43
  804.0 13.6 %fusion.43 = f32[2,2048,1792]{2,1,0:T(8,128)} fusion(bf16[2,2048,512]{1,2,0:T(8,128)(2,1)S(1)} %copy-done.12, bf16[2,512,1792]{2,1,0:T(8,128)(2,1)S(1)} %copy-done.46), kind=kOutput, calls=%fused_computation.129 | convolution fusion | flops 7516192768 | bytes 37224448 | tf_op jit(solution)/shard_map/erd,edf->erf/dot_general | solution.py:32
  817.5 16.5 %fusion.12 = f32[2,2048,1792]{2,1,0:T(8,128)} fusion(bf16[2,1792,512]{2,1,0:T(8,128)(2,1)} %param.28, bf16[2,2048,512]{2,1,0:T(8,128)(2,1)} %bitcast.157, f32[2,2048]{1,0:T(2,128)S(1)} %bitcast.168), kind=kOutput, calls=%fused_computation.47 | convolution fusion | flops 7522484224 | bytes 37240832 | tf_op jit(solution)/shard_map/erd,efd->erf/dot_general | solution.py:44
  834.0 40.2 %multiply_convert_fusion.1 = (bf16[2,2048,1792]{2,1,0:T(8,128)(2,1)}, bf16[2,2048,1792]{2,1,0:T(8,128)(2,1)}, bf16[2,2048,1792]{2,1,0:T(8,128)(2,1)}) fusion(f32[2,2048,1792]{2,1,0:T(8,128)} %fusion.43, f32[2,2048,1792]{2,1,0:T(8,128)} %fusion.12, bf16[2,2048,512]{1,2,0:T(8,128)(2,1)S(1)} %copy-done.13, bf16[2,512,1792]{2,1,0:T(8,128)(2,1)} %param.27), kind=kOutput, calls=%fused_computation.16 | convolution fusion | flops 7626293248 | bytes 110624768 | tf_op jit(solution)/shard_map/erd,edf->erf/dot_general | solution.py:33
  929.6 19.1 %copy.87 = bf16[2,2048,512]{2,0,1:T(2,128)(2,1)} copy(bf16[2,2048,512]{2,1,0:T(8,128)(2,1)S(1)} %add_convert_fusion) | data formatting | bytes 8388608 | tf_op jit(solution)/shard_map/convert_element_type | solution.py:50
  953.8 15.7 %fusion.46 = f32[2,512,1792]{2,1,0:T(8,128)} fusion(bf16[2,2048,512]{1,2,0:T(8,128)(2,1)} %all_to_all.187, bf16[2,2048,1792]{2,1,0:T(8,128)(2,1)} %get-tuple-element.50), kind=kOutput, calls=%fused_computation.132 | convolution fusion | flops 7516192768 | bytes 26214400 | tf_op jit(solution)/shard_map/erd,erf->edf/dot_general | solution.py:49
  969.5 13.6 %fusion.10 = f32[2,1792,512]{2,1,0:T(8,128)} fusion(bf16[2,2048,1792]{2,1,0:T(8,128)(2,1)} %get-tuple-element.48, bf16[2,2048,512]{2,1,0:T(8,128)(2,1)S(1)} %bitcast.159, f32[2,2048]{1,0:T(2,128)S(1)} %bitcast.169), kind=kOutput, calls=%fused_computation.46 | convolution fusion | flops 7522484224 | bytes 26230784 | tf_op jit(solution)/shard_map/erf,erd->efd/dot_general | solution.py:43
  (223 shorter events, 358.9 us)
Async XLA Ops:
  5.8 198.9 %copy-start.26 = (s32[1024]{0:T(1024)}, s32[1024]{0:T(1024)S(1)}, u32[]{:S(2)}) copy-start(s32[1024]{0:T(1024)S(1)} %get-tuple-element.64) | copy-start | bytes 12292
  10.1 18.0 %copy-start.22 = (s32[4096]{0:T(1024)}, s32[4096]{0:T(1024)S(1)}, u32[]{:S(2)}) copy-start(s32[4096]{0:T(1024)S(1)} %scatter_custom_fusion) | copy-start | bytes 49156
  10.2 18.0 %copy-start.30 = (pred[4096]{0:T(1024)(128)(4,1)}, pred[4096]{0:T(1024)(128)(4,1)S(1)}, u32[]{:S(2)}) copy-start(pred[4096]{0:T(1024)(128)(4,1)S(1)} %compare_and_fusion.1) | copy-start | bytes 12292
  10.8 17.3 %copy-start.20 = (s32[4096]{0:T(1024)}, s32[4096]{0:T(1024)S(1)}, u32[]{:S(2)}) copy-start(s32[4096]{0:T(1024)S(1)} %get-tuple-element.55) | copy-start | bytes 49156
  146.6 53.1 %all-to-all-start.1 = ((bf16[2,2048,512]{2,0,1:T(2,128)(2,1)}), bf16[2,2048,512]{2,0,1:T(2,128)(2,1)}, u32[]{:S(2)}, u32[]{:S(2)}) async-start(bf16[2,2048,512]{2,0,1:T(2,128)(2,1)} %copy.69), calls=%async_computation.1 | async-start | bytes 8388608 | tf_op jit(solution)/shard_map/all_to_all | solution.py:27
  152.2 25.9 %copy-start.24 = (s32[1024]{0:T(1024)}, s32[1024]{0:T(1024)S(1)}, u32[]{:S(2)}) copy-start(s32[1024]{0:T(1024)S(1)} %eq.58) | copy-start | bytes 12292
  152.9 63.3 %copy-start.18 = (f32[512,2]{1,0:T(8,128)}, f32[512,2]{1,0:T(8,128)S(1)}, u32[]{:S(2)}) copy-start(f32[512,2]{1,0:T(8,128)S(1)} %copy.64) | copy-start | bytes 12292
  155.7 22.4 %copy-start.32 = (s32[1024]{0:T(1024)}, s32[1024]{0:T(1024)S(1)}, u32[]{:S(2)}) copy-start(s32[1024]{0:T(1024)S(1)} %fusion.19) | copy-start | bytes 12292
  178.1 34.4 %copy-start.34 = (pred[1024]{0:T(1024)(128)(4,1)}, pred[1024]{0:T(1024)(128)(4,1)S(1)}, u32[]{:S(2)}) copy-start(pred[1024]{0:T(1024)(128)(4,1)S(1)} %compare_and_fusion.3) | copy-start | bytes 3076
  220.8 17.4 %copy-start.2 = (bf16[512,512]{1,0:T(8,128)(2,1)}, bf16[512,512]{1,0:T(8,128)(2,1)S(1)}, u32[]{:S(2)}) copy-start(bf16[512,512]{1,0:T(8,128)(2,1)S(1)} %add_convert_fusion.5) | copy-start | bytes 1572868
  294.8 52.9 %all-to-all-start.5 = ((bf16[8,512,512]{2,1,0:T(8,128)(2,1)}), bf16[8,512,512]{2,1,0:T(8,128)(2,1)}, u32[]{:S(2)}, u32[]{:S(2)}) async-start(bf16[8,512,512]{2,1,0:T(8,128)(2,1)} %bitcast.141), calls=%async_computation.5 | async-start | bytes 8388608 | tf_op jit(solution)/shard_map/all_to_all | solution.py:23
  300.0 16.9 %copy-start.16 = (f32[512,2]{1,0:T(8,128)}, f32[512,2]{1,0:T(8,128)S(1)}, u32[]{:S(2)}) copy-start(f32[512,2]{1,0:T(8,128)S(1)} %copy.71) | copy-start | bytes 12292
  347.7 50.7 %all-to-all-start.4 = ((f32[4,2,512]{2,1,0:T(2,128)}), f32[4,2,512]{2,1,0:T(2,128)S(1)}, u32[]{:S(2)}, u32[]{:S(2)}) async-start(f32[4,2,512]{2,1,0:T(2,128)} %all_to_all.171), calls=%async_computation.4 | async-start | bytes 32768 | tf_op jit(solution)/shard_map/all_to_all | solution.py:23
  398.4 41.9 %copy-start.37 = (f32[4,2,512]{2,1,0:T(2,128)}, f32[4,2,512]{2,1,0:T(2,128)S(1)}, u32[]{:S(2)}) copy-start(f32[4,2,512]{2,1,0:T(2,128)S(1)} %all-to-all-done.4) | copy-start | bytes 49156
  453.7 65.6 %all-to-all-start.12 = ((f32[2,4,512]{2,0,1:T(2,128)}), f32[2,4,512]{2,0,1:T(2,128)S(1)}, u32[]{:S(2)}, u32[]{:S(2)}) async-start(f32[2,4,512]{2,0,1:T(2,128)} %bitcast.43), calls=%async_computation.12 | async-start | bytes 32768 | tf_op jit(solution)/shard_map/all_to_all | solution.py:27
  519.3 53.2 %all-to-all-start.6 = ((bf16[2,2048,512]{2,0,1:T(2,128)(2,1)}), bf16[2,2048,512]{2,0,1:T(2,128)(2,1)}, u32[]{:S(2)}, u32[]{:S(2)}) async-start(bf16[2,2048,512]{2,0,1:T(2,128)(2,1)} %copy.80), calls=%async_computation.6 | async-start | bytes 8388608 | tf_op jit(solution)/shard_map/all_to_all | solution.py:27
  558.5 18.9 %copy-start.19 = (f32[512,2]{1,0:T(8,128)S(1)}, f32[512,2]{1,0:T(8,128)}, u32[]{:S(2)}) copy-start(f32[512,2]{1,0:T(8,128)} %copy-done.18) | copy-start | bytes 12292
  558.5 19.1 %copy-start.29 = (s32[4096]{0:T(1024)S(1)}, s32[4096]{0:T(1024)}, u32[]{:S(2)}) copy-start(s32[4096]{0:T(1024)} %get-tuple-element.54) | copy-start | bytes 49156
  572.5 52.8 %all-to-all-start.3 = ((bf16[2,2048,512]{2,0,1:T(2,128)(2,1)}), bf16[2,2048,512]{2,0,1:T(2,128)(2,1)}, u32[]{:S(2)}, u32[]{:S(2)}) async-start(bf16[2,2048,512]{2,0,1:T(2,128)(2,1)} %copy.76), calls=%async_computation.3 | async-start | bytes 8388608 | tf_op jit(solution)/shard_map/all_to_all | solution.py:27
  577.5 16.7 %copy-start.23 = (s32[4096]{0:T(1024)S(1)}, s32[4096]{0:T(1024)}, u32[]{:S(2)}) copy-start(s32[4096]{0:T(1024)} %copy-done.22) | copy-start | bytes 49156
  577.6 17.4 %copy-start.28 = (s32[1024]{0:T(1024)S(1)}, s32[1024]{0:T(1024)}, u32[]{:S(2)}) copy-start(s32[1024]{0:T(1024)} %get-tuple-element.62) | copy-start | bytes 12292
  647.4 17.4 %copy-start.4 = (bf16[512,512]{1,0:T(8,128)(2,1)}, bf16[512,512]{1,0:T(8,128)(2,1)S(1)}, u32[]{:S(2)}) copy-start(bf16[512,512]{1,0:T(8,128)(2,1)S(1)} %add_convert_fusion.3) | copy-start | bytes 1572868
  664.8 17.3 %copy-start.31 = (pred[4096]{0:T(1024)(128)(4,1)S(1)}, pred[4096]{0:T(1024)(128)(4,1)}, u32[]{:S(2)}) copy-start(pred[4096]{0:T(1024)(128)(4,1)} %copy-done.30) | copy-start | bytes 12292
  688.1 21.2 %slice-start = ((s8[14680064]{0:T(1024)(128)(4,1)}), s8[2097152]{0:T(1024)(128)(4,1)S(1)}, s32[]{:S(2)}) async-start(s8[14680064]{0:T(1024)(128)(4,1)} %bitcast.174), calls=%async_computation.13 | async-start | bytes 4194304
  688.1 53.0 %all-to-all-start.8 = ((bf16[8,512,512]{2,1,0:T(8,128)(2,1)}), bf16[8,512,512]{2,1,0:T(8,128)(2,1)}, u32[]{:S(2)}, u32[]{:S(2)}) async-start(bf16[8,512,512]{2,1,0:T(8,128)(2,1)} %bitcast.142), calls=%async_computation.8 | async-start | bytes 8388608 | tf_op jit(solution)/shard_map/all_to_all | solution.py:23
  693.3 16.0 %copy-start.11 = (bf16[2,4,512,512]{3,2,1,0:T(8,128)(2,1)S(1)}, bf16[2,4,512,512]{3,2,1,0:T(8,128)(2,1)}, u32[]{:S(2)}) copy-start(bf16[2,4,512,512]{3,2,1,0:T(8,128)(2,1)} %copy.75) | copy-start | bytes 12582916
  741.1 53.1 %all-to-all-start.9 = ((bf16[8,512,512]{2,1,0:T(8,128)(2,1)}), bf16[8,512,512]{2,1,0:T(8,128)(2,1)}, u32[]{:S(2)}, u32[]{:S(2)}) async-start(bf16[8,512,512]{2,1,0:T(8,128)(2,1)} %bitcast.140), calls=%async_computation.9 | async-start | bytes 8388608 | tf_op jit(solution)/shard_map/all_to_all | solution.py:23
  794.2 23.3 %all-to-all-start.7 = ((f32[4,2,512]{2,1,0:T(2,128)}), f32[4,2,512]{2,1,0:T(2,128)S(1)}, u32[]{:S(2)}, u32[]{:S(2)}) async-start(f32[4,2,512]{2,1,0:T(2,128)} %all_to_all.181), calls=%async_computation.7 | async-start | bytes 32768 | tf_op jit(solution)/shard_map/all_to_all | solution.py:23
  817.5 16.5 %copy-start.39 = (f32[4,2,512]{2,1,0:T(2,128)}, f32[4,2,512]{2,1,0:T(2,128)S(1)}, u32[]{:S(2)}) copy-start(f32[4,2,512]{2,1,0:T(2,128)S(1)} %all-to-all-done.7) | copy-start | bytes 49156
  817.5 16.5 %copy-start.13 = (bf16[2,2048,512]{1,2,0:T(8,128)(2,1)S(1)}, bf16[2,2048,512]{1,2,0:T(8,128)(2,1)}, u32[]{:S(2)}) copy-start(bf16[2,2048,512]{1,2,0:T(8,128)(2,1)} %all_to_all.187) | copy-start | bytes 12582916
  912.8 35.8 %all-to-all-start.11 = ((f32[2,4,512]{2,0,1:T(2,128)}), f32[2,4,512]{2,0,1:T(2,128)S(1)}, u32[]{:S(2)}, u32[]{:S(2)}) async-start(f32[2,4,512]{2,0,1:T(2,128)} %bitcast.41), calls=%async_computation.11 | async-start | bytes 32768 | tf_op jit(solution)/shard_map/all_to_all | solution.py:27
  948.7 53.0 %all-to-all-start.10 = ((bf16[2,2048,512]{2,0,1:T(2,128)(2,1)}), bf16[2,2048,512]{2,0,1:T(2,128)(2,1)}, u32[]{:S(2)}, u32[]{:S(2)}) async-start(bf16[2,2048,512]{2,0,1:T(2,128)(2,1)} %copy.87), calls=%async_computation.10 | async-start | bytes 8388608 | tf_op jit(solution)/shard_map/all_to_all | solution.py:27
  (33 other events, 315.5 us)
where the time goes:
time: 1030 us; the launch traced here: 1020 us
  matrix products  407 us (40%)
  local copies, waits for them, and re-layouts  300 us (29%)
  waiting for transfers between devices  116 us (11%)
  blocking collectives  104 us (10%)
  starting transfers between devices  49.8 us (5%)
  other arithmetic  45.9 us (4%)
    gather x7, local copies, waits for them, and re-layouts, send_rows(): send_buf = jnp.take(rows, index, axis=0, mode='fill', fill_value=0)  120 us
    all_to_all x2, blocking collectives, send_rows(): return lax.all_to_all(send_buf, 'ep', 0, 1, tiled=True)  104 us
    dot_general x4, matrix products, expert_forward(): jnp.einsum('erd,edf->erf', u_rows, w_up, preferred_element_type=jnp.float32)  81.1 us
    dot_general x4, matrix products, expert_forward(): jnp.einsum('erf,efd->erd', hidden, w_down, preferred_element_type=jnp.flo...  73 us
    all_to_all x6, waiting for transfers between devices, send_back(): back_rows = lax.all_to_all(rows, 'ep', 1, 0, tiled=True)  59.5 us
    dot_general x2, matrix products, expert_backward(): jnp.einsum('erd,efd->erf', d_out, w_down, preferred_element_type=jnp.floa...  58.4 us
    dot_general x4, matrix products, expert_forward(): jnp.einsum('erd,edf->erf', u_rows, w_gate, preferred_element_type=jnp.flo...  56.5 us
    all_to_all x5, waiting for transfers between devices, send_rows(): return lax.all_to_all(send_buf, 'ep', 0, 1, tiled=True)  56.3 us
  transfers between devices with their start and end apart: 11, of which 7 were waited for; matrix products, arithmetic and copies ran while one was open for 36% of the time, Pallas kernels for 0%

commit v1 on v0

v1 whole, which is shorter than its diff:
```python
import functools

import jax
import jax.numpy as jnp
from jax import lax
from jax.experimental import pallas as pl
from jax.experimental.pallas import tpu as pltpu
from jax.sharding import PartitionSpec as P

ROWS = 256
TOKS = 256
COLS = 256
VMEM = 66_000_000

BF = jnp.bfloat16
F32 = jnp.float32


def mm(a, b):
    return lax.dot_general(a, b, (((1,), (0,)), ((), ())), preferred_element_type=F32)


def mm_nt(a, b):
    return lax.dot_general(a, b, (((1,), (1,)), ((), ())), preferred_element_type=F32)


def mm_tn(a, b):
    return lax.dot_general(a, b, (((0,), (0,)), ((), ())), preferred_element_type=F32)


def pick_rows(slot_row, base):
    want = lax.broadcasted_iota(jnp.int32, (ROWS, TOKS), 0) + base
    return slot_row == want


def pick_toks(slot_col, base):
    want = lax.broadcasted_iota(jnp.int32, (TOKS, ROWS), 1) + base
    return slot_col == want


def for_blocks(starts_ref, e, base, blocks, body):
    def step(b, carry):
        lo = starts_ref[e, b]
        hi = starts_ref[e, b + 1]

        @pl.when((lo < base + ROWS) & (hi > base) & (hi > lo))
        def _():
            body(b)

        return carry

    lax.fori_loop(0, blocks, step, 0)


def forward_kernel(starts_ref, x_ref, slot_row_ref, slot_col_ref, gate_col_ref, w1_ref, w3_ref, w2_ref, y_ref, u_acc, h_ref):
    e = pl.program_id(0)
    blocks = x_ref.shape[0] // TOKS
    width = w1_ref.shape[2]

    @pl.when(e == 0)
    def _():
        y_ref[...] = jnp.zeros_like(y_ref)

    def tile(k, carry):
        base = k * ROWS
        u_acc[...] = jnp.zeros_like(u_acc)

        def take(b):
            toks = pl.ds(pl.multiple_of(b * TOKS, TOKS), TOKS)
            hot = pick_rows(slot_row_ref[0, b], base).astype(F32).astype(BF)
            u_acc[...] += mm(hot, x_ref[toks, :])

        for_blocks(starts_ref, e, base, blocks, take)
        u = u_acc[...].astype(BF)
        for c in range(0, width, COLS):
            cols = slice(c, c + COLS)
            a = mm(u, w1_ref[0, :, cols])
            b = mm(u, w3_ref[0, :, cols])
            h_ref[:, cols] = (a * jax.nn.sigmoid(a) * b).astype(BF)
        o = mm(h_ref[...], w2_ref[0]).astype(BF)

        def give(b):
            toks = pl.ds(pl.multiple_of(b * TOKS, TOKS), TOKS)
            hot = pick_toks(slot_col_ref[0, toks, :], base).astype(F32).astype(BF)
            y_ref[toks, :] += gate_col_ref[0, toks, :] * mm(hot, o)

        for_blocks(starts_ref, e, base, blocks, give)
        return carry

    count = starts_ref[e, blocks]
    lax.fori_loop(0, (count + ROWS - 1) // ROWS, tile, 0)


def backward_kernel(starts_ref, x_ref, dy_ref, slot_row_ref, slot_col_ref, gate_row_ref, w1_ref, w3_ref, w2_ref,
                    dx_ref, dg_ref, dw1_ref, dw3_ref, dw2_ref, u_acc, dy_acc, g_acc, h_ref, da_ref, db_ref):
    e = pl.program_id(0)
    blocks = x_ref.shape[0] // TOKS
    width = w1_ref.shape[2]

    @pl.when(e == 0)
    def _():
        dx_ref[...] = jnp.zeros_like(dx_ref)

    dg_ref[...] = jnp.zeros_like(dg_ref)
    dw1_ref[...] = jnp.zeros_like(dw1_ref)
    dw3_ref[...] = jnp.zeros_like(dw3_ref)
    dw2_ref[...] = jnp.zeros_like(dw2_ref)

    def tile(k, carry):
        base = k * ROWS
        u_acc[...] = jnp.zeros_like(u_acc)
        dy_acc[...] = jnp.zeros_like(dy_acc)
        g_acc[...] = jnp.zeros_like(g_acc)

        def take(b):
            toks = pl.ds(pl.multiple_of(b * TOKS, TOKS), TOKS)
            pick = pick_rows(slot_row_ref[0, b], base)
            hot = pick.astype(F32).astype(BF)
            u_acc[...] += mm(hot, x_ref[toks, :])
            dy_acc[...] += mm(hot, dy_ref[toks, :])
            g_acc[...] += jnp.sum(jnp.where(pick, gate_row_ref[0, b], 0.0), axis=1, keepdims=True)

        for_blocks(starts_ref, e, base, blocks, take)
        u = u_acc[...].astype(BF)
        q = (g_acc[...] * dy_acc[...]).astype(BF)
        for c in range(0, width, COLS):
            cols = slice(c, c + COLS)
            a = mm(u, w1_ref[0, :, cols])
            b = mm(u, w3_ref[0, :, cols])
            dh = mm_nt(q, w2_ref[0, cols, :])
            s = jax.nn.sigmoid(a)
            act = a * s
            h_ref[:, cols] = (act * b).astype(BF)
            da_ref[:, cols] = (dh * b * s * (1.0 + a * (1.0 - s))).astype(BF)
            db_ref[:, cols] = (dh * act).astype(BF)
        o = mm(h_ref[...], w2_ref[0]).astype(BF)
        dgate = jnp.sum(dy_acc[...] * o.astype(F32), axis=1, keepdims=True)
        for c in range(0, width, COLS):
            cols = slice(c, c + COLS)
            dw2_ref[0, cols, :] += mm_tn(h_ref[:, cols], q)
            dw1_ref[0, :, cols] += mm_tn(u, da_ref[:, cols])
            dw3_ref[0, :, cols] += mm_tn(u, db_ref[:, cols])
        du = (mm_nt(da_ref[...], w1_ref[0]) + mm_nt(db_ref[...], w3_ref[0])).astype(BF)

        def give(b):
            toks = pl.ds(pl.multiple_of(b * TOKS, TOKS), TOKS)
            hot = pick_toks(slot_col_ref[0, toks, :], base).astype(F32).astype(BF)
            dx_ref[toks, :] += mm(hot, du)
            pick = pick_rows(slot_row_ref[0, b], base)
            dg_ref[0, b] += jnp.sum(jnp.where(pick, dgate, 0.0), axis=0, keepdims=True)

        for_blocks(starts_ref, e, base, blocks, give)
        return carry

    count = starts_ref[e, blocks]
    lax.fori_loop(0, (count + ROWS - 1) // ROWS, tile, 0)


def whole(shape):
    return pl.BlockSpec(shape, lambda e, *_: (0,) * len(shape), pipeline_mode=pl.Buffered(1))


def per_expert(shape):
    return pl.BlockSpec((1,) + shape, lambda e, *_: (e,) + (0,) * len(shape))


def run_forward(x, maps, w1, w3, w2):
    tokens, dim = x.shape
    experts, _, width = w1.shape
    blocks = tokens // TOKS
    return pl.pallas_call(
        forward_kernel,
        grid_spec=pltpu.PrefetchScalarGridSpec(
            num_scalar_prefetch=1,
            grid=(experts,),
            in_specs=[
                whole((tokens, dim)),
                per_expert((blocks, 1, TOKS)),
                per_expert((tokens, 1)),
                per_expert((tokens, 1)),
                per_expert((dim, width)),
                per_expert((dim, width)),
                per_expert((width, dim)),
            ],
            out_specs=whole((tokens, dim)),
            scratch_shapes=[pltpu.VMEM((ROWS, dim), F32), pltpu.VMEM((ROWS, width), BF)],
        ),
        out_shape=jax.ShapeDtypeStruct((tokens, dim), F32),
        compiler_params=pltpu.CompilerParams(vmem_limit_bytes=VMEM),
        cost_estimate=pl.CostEstimate(flops=6 * tokens * dim * width, bytes_accessed=6 * experts * dim * width, transcendentals=0),
        name="expert_forward",
    )(maps["starts"], x, maps["slot_row"], maps["slot_col"], maps["gate_col"], w1, w3, w2)


def run_backward(x, dy, maps, w1, w3, w2):
    tokens, dim = x.shape
    experts, _, width = w1.shape
    blocks = tokens // TOKS
    return pl.pallas_call(
        backward_kernel,
        grid_spec=pltpu.PrefetchScalarGridSpec(
            num_scalar_prefetch=1,
            grid=(experts,),
            in_specs=[
                whole((tokens, dim)),
                whole((tokens, dim)),
                per_expert((blocks, 1, TOKS)),
                per_expert((tokens, 1)),
                per_expert((blocks, 1, TOKS)),
                per_expert((dim, width)),
                per_expert((dim, width)),
                per_expert((width, dim)),
            ],
            out_specs=[
                whole((tokens, dim)),
                per_expert((blocks, 1, TOKS)),
                pl.BlockSpec((1, dim, width), lambda e, *_: (e, 0, 0), pipeline_mode=pl.Buffered(1)),
                pl.BlockSpec((1, dim, width), lambda e, *_: (e, 0, 0), pipeline_mode=pl.Buffered(1)),
                pl.BlockSpec((1, width, dim), lambda e, *_: (e, 0, 0), pipeline_mode=pl.Buffered(1)),
            ],
            scratch_shapes=[
                pltpu.VMEM((ROWS, dim), F32),
                pltpu.VMEM((ROWS, dim), F32),
                pltpu.VMEM((ROWS, 1), F32),
                pltpu.VMEM((ROWS, width), BF),
                pltpu.VMEM((ROWS, width), BF),
                pltpu.VMEM((ROWS, width), BF),
            ],
        ),
        out_shape=[
            jax.ShapeDtypeStruct((tokens, dim), F32),
            jax.ShapeDtypeStruct((experts, blocks, 1, TOKS), F32),
            jax.ShapeDtypeStruct((experts, dim, width), F32),
            jax.ShapeDtypeStruct((experts, dim, width), F32),
            jax.ShapeDtypeStruct((experts, width, dim), F32),
        ],
        compiler_params=pltpu.CompilerParams(vmem_limit_bytes=VMEM),
        cost_estimate=pl.CostEstimate(flops=18 * tokens * dim * width, bytes_accessed=18 * experts * dim * width, transcendentals=0),
        name="expert_backward",
    )(maps["starts"], x, dy, maps["slot_row"], maps["slot_col"], maps["gate_row"], w1, w3, w2)


def routing(ids, gates, first, experts):
    tokens = ids.shape[0]
    blocks = tokens // TOKS
    hits = ids.T[None, :, :] == (first + jnp.arange(experts, dtype=jnp.int32))[:, None, None]
    mask = jnp.any(hits, axis=1)
    gate = jnp.sum(jnp.where(hits, gates.T[None], 0.0), axis=1)
    seen = jnp.cumsum(mask.astype(jnp.int32), axis=1)
    slot = jnp.where(mask, seen - 1, -1)
    starts = jnp.concatenate([jnp.zeros((experts, 1), jnp.int32), seen[:, TOKS - 1 :: TOKS]], axis=1)
    return {
        "hits": hits,
        "starts": starts,
        "slot_row": slot.reshape(experts, blocks, 1, TOKS),
        "slot_col": slot[:, :, None],
        "gate_row": gate.reshape(experts, blocks, 1, TOKS),
        "gate_col": gate[:, :, None],
    }


def solution(mesh):
    tok_spec = P(("dp", "ep"))
    w_spec = P("ep")

    def device_program(x_in, idx_a, idx_b, gate_a, gate_b, dy_out, w1_a, w3_a, w2_a, w1_b, w3_b, w2_b):
        experts = w1_a.shape[0]
        first = lax.axis_index("ep").astype(jnp.int32) * experts
        gather = functools.partial(lax.all_gather, axis_name="ep", tiled=True)
        scatter = functools.partial(lax.psum_scatter, axis_name="ep", tiled=True)

        ids = gather(jnp.concatenate([idx_a, idx_b], axis=1))
        gates = gather(jnp.concatenate([gate_a, gate_b], axis=1))
        maps_a = routing(ids[:, :2], gates[:, :2], first, experts)
        maps_b = routing(ids[:, 2:], gates[:, 2:], first, experts)

        def forward(x_own, x_all, maps, w1, w3, w2):
            part = run_forward(x_all, maps, w1, w3, w2)
            return (x_own.astype(F32) + scatter(part)).astype(BF)

        def backward(dy_own, dy_all, x_all, maps, w1, w3, w2):
            part, dg, dw1, dw3, dw2 = run_backward(x_all, dy_all, maps, w1, w3, w2)
            dx = (dy_own.astype(F32) + scatter(part)).astype(BF)
            dg = dg.reshape(experts, 1, -1)
            dgate = scatter(jnp.sum(jnp.where(maps["hits"], dg, 0.0), axis=0).T)
            return dx, dgate, (dw1, dw3, dw2)

        x_all = gather(x_in)
        x_mid = forward(x_in, x_all, maps_a, w1_a, w3_a, w2_a)
        mid_all = gather(x_mid)
        dy_all = gather(dy_out)
        x_out = forward(x_mid, mid_all, maps_b, w1_b, w3_b, w2_b)
        dx_mid, dgate_b, grads_b = backward(dy_out, dy_all, mid_all, maps_b, w1_b, w3_b, w2_b)
        x_again, dx_mid_again = lax.optimization_barrier((x_in, dx_mid))
        dx_in, dgate_a, grads_a = backward(dx_mid, gather(dx_mid_again), gather(x_again), maps_a, w1_a, w3_a, w2_a)
        return (x_out, dx_in) + grads_a + grads_b + (dgate_a, dgate_b)

    return jax.shard_map(device_program, mesh=mesh, in_specs=(tok_spec,) * 6 + (w_spec,) * 6, out_specs=(tok_spec,) * 10, check_vma=False)
```

time: 1030 us -> 480 us (0.47)
  matrix products: 407 us -> 0 us
  local copies, waits for them, and re-layouts: 300 us -> 19.1 us
  waiting for transfers between devices: 116 us -> 268 us
  Pallas kernels: 0 us -> 143 us
  blocking collectives: 104 us -> 17 us
  starting transfers between devices: 49.8 us -> 0.85 us
  other arithmetic: 45.9 us -> 16.8 us
  between operations: 1.79 us -> 14.1 us
    dot_general x24 -> x0, matrix products: 407 us -> none  [the longest x4 81.1 us: expert_forward(): jnp.einsum('erd,edf->erf', u_rows, w_up, preferred_element_type=jnp.float32)]
    gather x13 -> x0, local copies, waits for them, and re-layouts: 163 us -> none  [the longest x7 120 us: send_rows(): send_buf = jnp.take(rows, index, axis=0, mode='fill', fill_value=0)]
    reduce_scatter x0 -> x4, waiting for transfers between devices: none -> 156 us  [the longest x2 107 us: backward(): dx = (dy_own.astype(F32) + scatter(part)).astype(BF)]
    pallas_call x0 -> x4, Pallas kernels: none -> 143 us  [the longest x2 94.6 us: run_backward(): pl.pallas_call(backward_kernel, grid_spec=pltpu.PrefetchScalarGridSpec(nu...]
    all_to_all x11 -> x0, waiting for transfers between devices: 116 us -> none  [the longest x6 59.5 us: send_back(): back_rows = lax.all_to_all(rows, 'ep', 1, 0, tiled=True)]
    all_to_all x2 -> x0, blocking collectives: 104 us -> none  [send_rows(): return lax.all_to_all(send_buf, 'ep', 0, 1, tiled=True)]
    convert_element_type x8 -> x0, local copies, waits for them, and re-layouts: 67.4 us -> none  [the longest x2 38.1 us: expert_backward(): (jnp.einsum('erf,edf->erd', d_pre_gate, w_gate, preferred_element_type=jn...]
    unnamed x0 -> x13, waiting for transfers between devices: none -> 66.7 us
  transfers between devices with their start and end apart: 11 -> 11, of which waited for: 7 -> 8; matrix products, arithmetic and copies ran while one was open for 36% -> 7% of each run, Pallas kernels for 0% -> 15%
where the time goes in v1:
time: 480 us; the launch traced here: 479 us
  waiting for transfers between devices  268 us (56%)
  Pallas kernels  143 us (30%)
  local copies, waits for them, and re-layouts  19.1 us (4%)
  blocking collectives  17 us (4%)
  other arithmetic  16.8 us (4%)
  between operations  14.1 us (3%)
    reduce_scatter x2, waiting for transfers between devices, backward(): dx = (dy_own.astype(F32) + scatter(part)).astype(BF)  107 us
    pallas_call x2, Pallas kernels, run_backward(): pl.pallas_call(backward_kernel, grid_spec=pltpu.PrefetchScalarGridSpec(nu...  94.6 us
    unnamed x13, waiting for transfers between devices  66.7 us
    reduce_scatter x2, waiting for transfers between devices, forward(): return (x_own.astype(F32) + scatter(part)).astype(BF)  49.2 us
    pallas_call x2, Pallas kernels, run_forward(): pl.pallas_call(forward_kernel, grid_spec=pltpu.PrefetchScalarGridSpec(num...  48.3 us
    all_gather x1, waiting for transfers between devices, device_program(): mid_all = gather(x_mid)  21.5 us
    all_gather x1, waiting for transfers between devices, device_program(): gather(dx_mid_again)  12.9 us
    all_gather x1, waiting for transfers between devices, device_program(): dy_all = gather(dy_out)  11.3 us
  transfers between devices with their start and end apart: 11, of which 8 were waited for; matrix products, arithmetic and copies ran while one was open for 7% of the time, Pallas kernels for 15%

profile of v1, /device:TPU:0, one launch (start us, length us, event | category | flops | bytes accessed | tf_op | source)
XLA Modules:
  0.0 479.2 jit_solution(8398256734002285019)
XLA Ops:
  8.0 0.7 pad_add_fusion
  8.7 10.0 %all_gather.21 = s32[2048,4]{0,1:T(4,128)S(1)} all-gather(s32[512,4]{0,1:T(4,128)S(1)} %pad_add_fusion), channel_id=1, replica_groups=mesh['dp'=2,'ep'=4] {'ep'}, dimensions={0}, use_global_device_ids=true | all-gather | bytes 40960 | tf_op jit(solution)/shard_map/all_gather | solution.py:272
  20.7 0.8 copy.47
  21.6 1.9 sub.20
  23.6 7.0 %all_gather.23 = f32[2048,4]{0,1:T(4,128)S(1)} all-gather(f32[512,4]{0,1:T(4,128)S(1)} %pad_maximum_fusion), channel_id=1, replica_groups=mesh['dp'=2,'ep'=4] {'ep'}, dimensions={0}, use_global_device_ids=true | all-gather | bytes 40960 | tf_op jit(solution)/shard_map/all_gather | solution.py:273
  30.8 2.0 copy.49.gate_col_ref
  33.4 1.6 broadcast_select_fusion.1.slot_col_ref
  35.0 24.2 %expert_forward.2 = f32[2048,512]{1,0:T(8,128)} custom-call(s32[2,9]{1,0:T(2,128)} %concatenate.13.starts_ref, bf16[2048,512]{1,0:T(8,128)(2,1)} %all-gather.6.cloned.1.call-done.x_ref, s32[2,8,1,256]{3,2,1,0:T(1,128)} %broadcast_select_fusion.3.slot_row_ref, s32[2,2048,1]{2,1,0:T(8,128)} %broadcast_select_fusion.1.slot_col_ref, ...), custom_call_target="tpu_custom_call" | custom-call | flops 11274289152 | bytes 11010048 | tf_op jit(solution)/shard_map/expert_forward/pallas_call | solution.py:171
  60.0 49.2 %reduce-scatter.11.cloned.1.call-done = f32[512,512]{1,0:T(8,128)} async-done(((f32[2048,512]{1,0:T(8,128)}), f32[512,512]{1,0:T(8,128)}) %reduce-scatter.11.cloned.1.call-update) | async-done | bytes 1048592 | tf_op jit(solution)/shard_map/reduce_scatter | solution.py:279
  109.1 2.2 add_convert_fusion.3
  114.0 0.8 copy.51
  114.8 1.9 sub.21
  117.4 1.5 broadcast_select_fusion.slot_col_ref
  119.0 11.3 %all-gather.10.cloned.1.call-done.dy_ref = bf16[2048,512]{1,0:T(8,128)(2,1)} async-done(((bf16[512,512]{1,0:T(8,128)(2,1)}), bf16[2048,512]{1,0:T(8,128)(2,1)}) %all-gather.10.cloned.1.call-update) | async-done | bytes 2097168 | tf_op jit(solution)/shard_map/all_gather | solution.py:291
  130.3 21.5 %all-gather.8.cloned.1.call-done.x_ref = bf16[2048,512]{1,0:T(8,128)(2,1)} async-done(((bf16[512,512]{1,0:T(8,128)(2,1)}), bf16[2048,512]{1,0:T(8,128)(2,1)}) %all-gather.8.cloned.1.call-update) | async-done | bytes 2097168 | tf_op jit(solution)/shard_map/all_gather | solution.py:290
  151.8 47.3 %expert_backward.2 = (f32[2048,512]{1,0:T(8,128)}, f32[2,8,1,256]{3,2,1,0:T(1,128)}, f32[2,512,1792]{2,1,0:T(8,128)}, f32[2,512,1792]{2,1,0:T(8,128)}, f32[2,1792,512]{2,1,0:T(8,128)}) custom-call(s32[2,9]{1,0:T(2,128)} %concatenate.15.starts_ref, bf16[2048,512]{1,0:T(8,128)(2,1)} %all-gather.8.cloned.1.call-done.x_ref, ...), custom_call_target="tpu_custom_call" | custom-call | flops 33822867456 | bytes 33030144 | tf_op jit(solution)/shard_map/expert_backward/pallas_call | solution.py:199
  199.2 67.8 %reduce-scatter.15.cloned.1.call-done = f32[512,512]{1,0:T(8,128)} async-done(((f32[2048,512]{1,0:T(8,128)}), f32[512,512]{1,0:T(8,128)}) %reduce-scatter.15.cloned.1.call-update) | async-done | bytes 1048592 | tf_op jit(solution)/shard_map/reduce_scatter | solution.py:283
  266.9 2.2 add_convert_fusion.1
  269.9 2.0 copy.53.gate_col_ref
  271.9 24.2 %expert_forward.3 = f32[2048,512]{1,0:T(8,128)} custom-call(s32[2,9]{1,0:T(2,128)} %concatenate.15.starts_ref, bf16[2048,512]{1,0:T(8,128)(2,1)} %all-gather.8.cloned.1.call-done.x_ref, s32[2,8,1,256]{3,2,1,0:T(1,128)} %broadcast_select_fusion.2.slot_row_ref, s32[2,2048,1]{2,1,0:T(8,128)} %broadcast_select_fusion.slot_col_ref, ...), custom_call_target="tpu_custom_call" | custom-call | flops 11274289152 | bytes 11010048 | tf_op jit(solution)/shard_map/expert_forward/pallas_call | solution.py:171
  297.1 12.9 %all-gather.14.cloned.1.call-done.dy_ref = bf16[2048,512]{1,0:T(8,128)(2,1)} async-done(((bf16[512,512]{1,0:T(8,128)(2,1)}), bf16[2048,512]{1,0:T(8,128)(2,1)}) %all-gather.14.cloned.1.call-update) | async-done | bytes 2097168 | tf_op jit(solution)/shard_map/all_gather | solution.py:295
  309.9 47.3 %expert_backward.3 = (f32[2048,512]{1,0:T(8,128)}, f32[2,8,1,256]{3,2,1,0:T(1,128)}, f32[2,512,1792]{2,1,0:T(8,128)}, f32[2,512,1792]{2,1,0:T(8,128)}, f32[2,1792,512]{2,1,0:T(8,128)}) custom-call(s32[2,9]{1,0:T(2,128)} %concatenate.13.starts_ref, bf16[2048,512]{1,0:T(8,128)(2,1)} %all-gather.12.cloned.1.call-done.x_ref, ...), custom_call_target="tpu_custom_call" | custom-call | flops 33822867456 | bytes 33030144 | tf_op jit(solution)/shard_map/expert_backward/pallas_call | solution.py:199
  357.2 0.8 reduce.2
  358.1 1.4 copy.54
  359.5 1.4 copy.56
  362.0 2.2 add_convert_fusion.2
  364.2 44.0 %reduce-scatter.19.cloned.1.call-done = f32[512,2]{1,0:T(8,128)} async-done(((f32[2048,2]{1,0:T(8,128)}), f32[512,2]{1,0:T(8,128)}) %reduce-scatter.19.cloned.1.call-update) | async-done | bytes 4112
  408.2 1.7 copy.55
  409.8 19.9 %reduce-scatter.21.cloned.1.call-done = f32[512,2]{1,0:T(8,128)} async-done(((f32[2048,2]{1,0:T(8,128)}), f32[512,2]{1,0:T(8,128)}) %reduce-scatter.21.cloned.1.call-update) | async-done | bytes 4112
  429.7 1.7 copy.57
  431.3 39.1 %reduce-scatter.17.cloned.1.call-done = f32[512,512]{1,0:T(8,128)} async-done(((f32[2048,512]{1,0:T(8,128)}), f32[512,512]{1,0:T(8,128)}) %reduce-scatter.17.cloned.1.call-update) | async-done | bytes 1048592 | tf_op jit(solution)/shard_map/reduce_scatter | solution.py:283
  470.5 2.2 add_convert_fusion
  (72 shorter events, 10.8 us)
Async XLA Ops:
  7.2 16.4 %copy-start.5 = (f32[512,2]{0,1:T(2,128)S(1)}, f32[512,2]{0,1:T(2,128)}, u32[]{:S(2)}) copy-start(f32[512,2]{0,1:T(2,128)} %param.16) | copy-start | bytes 12292
  7.2 16.4 %copy-start.6 = (f32[512,2]{0,1:T(2,128)S(1)}, f32[512,2]{0,1:T(2,128)}, u32[]{:S(2)}) copy-start(f32[512,2]{0,1:T(2,128)} %param.15) | copy-start | bytes 12292
  7.2 27.8 %all-gather.6.cloned.1.call-start = ((), (), s32[]{:S(2)}) async-start(), calls=%async_computation.6 | async-start | bytes 2621440 | tf_op jit(solution)/shard_map/all_gather | solution.py:288
  7.9 101.2 %reduce-scatter.11.cloned.1.call-start = ((), (), s32[]{:S(2)}) async-start(), calls=%async_computation.7 | async-start | bytes 5242880 | tf_op jit(solution)/shard_map/reduce_scatter | solution.py:279
  59.2 50.0 %copy-start = (bf16[512,512]{1,0:T(8,128)(2,1)S(1)}, bf16[512,512]{1,0:T(8,128)(2,1)}, u32[]{:S(2)}) copy-start(bf16[512,512]{1,0:T(8,128)(2,1)} %param.12) | copy-start | bytes 1572868
  59.2 71.1 %all-gather.10.cloned.1.call-start = ((), (), s32[]{:S(2)}) async-start(), calls=%async_computation.10 | async-start | bytes 2621440 | tf_op jit(solution)/shard_map/all_gather | solution.py:291
  59.9 91.9 %all-gather.8.cloned.1.call-start = ((), (), s32[]{:S(2)}) async-start(), calls=%async_computation.8 | async-start | bytes 2621440 | tf_op jit(solution)/shard_map/all_gather | solution.py:290
  111.3 155.6 %reduce-scatter.15.cloned.1.call-start = ((), (), s32[]{:S(2)}) async-start(), calls=%async_computation.11 | async-start | bytes 5242880 | tf_op jit(solution)/shard_map/reduce_scatter | solution.py:283
  199.1 67.8 %copy-start.3 = (bf16[512,512]{1,0:T(8,128)(2,1)S(1)}, bf16[512,512]{1,0:T(8,128)(2,1)}, u32[]{:S(2)}) copy-start(bf16[512,512]{1,0:T(8,128)(2,1)} %param.17) | copy-start | bytes 1572868
  199.1 97.9 %all-gather.12.cloned.1.call-start = ((), (), s32[]{:S(2)}) async-start(), calls=%async_computation.12 | async-start | bytes 2621440 | tf_op jit(solution)/shard_map/all_gather | solution.py:295
  269.1 40.8 %all-gather.14.cloned.1.call-start = ((), (), s32[]{:S(2)}) async-start(), calls=%async_computation.13 | async-start | bytes 2621440 | tf_op jit(solution)/shard_map/all_gather | solution.py:295
  269.9 91.8 %reduce-scatter.13.cloned.1.call-start = ((), (), s32[]{:S(2)}) async-start(), calls=%async_computation.9 | async-start | bytes 5242880 | tf_op jit(solution)/shard_map/reduce_scatter | solution.py:279
  296.0 0.9 copy-start.4
  296.1 112.1 %reduce-scatter.19.cloned.1.call-start = ((), (), s32[]{:S(2)}) async-start(), calls=%async_computation.15 | async-start | bytes 1310720
  359.5 70.2 %reduce-scatter.21.cloned.1.call-start = ((), (), s32[]{:S(2)}) async-start(), calls=%async_computation.16 | async-start | bytes 1310720
  360.9 109.5 %reduce-scatter.17.cloned.1.call-start = ((), (), s32[]{:S(2)}) async-start(), calls=%async_computation.14 | async-start | bytes 5242880 | tf_op jit(solution)/shard_map/reduce_scatter | solution.py:283
  361.0 1.0 copy-start.1
  361.7 108.8 %copy-start.2 = (bf16[512,512]{1,0:T(8,128)(2,1)S(1)}, bf16[512,512]{1,0:T(8,128)(2,1)}, u32[]{:S(2)}) copy-start(bf16[512,512]{1,0:T(8,128)(2,1)} %add_convert_fusion.1) | copy-start | bytes 1572868
Sparse Core Ops, SparseCore 0:
  9.5 22.8 all-gather.5
  59.3 49.7 reduce-scatter.10
  110.7 19.5 all-gather.9
  132.2 19.5 all-gather.7
  199.2 67.6 reduce-scatter.14
  269.2 19.5 all-gather.11
  290.3 19.5 all-gather.13
  312.4 38.2 reduce-scatter.12
  359.6 48.5 reduce-scatter.18
  410.5 19.1 reduce-scatter.20
  432.2 38.2 reduce-scatter.16

commit v2 on v0

v2 whole, which is shorter than its diff:
```python
import jax
import jax.numpy as jnp
from jax import lax
from jax.experimental import pallas as pl
from jax.experimental.pallas import tpu as pltpu
from jax.sharding import PartitionSpec as P


ROWS = 256
TOKS = 256
SPAN = TOKS + 16
COLS = 256
EXPERTS = 2
VMEM = 66_000_000

BF = jnp.bfloat16
F32 = jnp.float32


def mm(a, b):
    return lax.dot_general(a, b, (((1,), (0,)), ((), ())), preferred_element_type=F32)


def mm_nt(a, b):
    return lax.dot_general(a, b, (((1,), (1,)), ((), ())), preferred_element_type=F32)


def mm_tn(a, b):
    return lax.dot_general(a, b, (((0,), (0,)), ((), ())), preferred_element_type=F32)


def block_of(refs, b):
    per = refs[0].shape[0] // TOKS
    return refs[b // per], slice((b % per) * TOKS, (b % per + 1) * TOKS)


def tile_rows(k):
    return pl.ds(pl.multiple_of(k * ROWS, ROWS), ROWS)


class Slots:
    def __init__(self, layer, starts_ref, rows_ref, cols_ref, blocks):
        self.line = layer * EXPERTS
        self.starts_ref, self.rows_ref, self.cols_ref, self.blocks = starts_ref, rows_ref, cols_ref, blocks

    def tiles(self, e):
        return (self.starts_ref[self.line + e, self.blocks] + ROWS - 1) // ROWS

    def base(self, e, b):
        return pl.multiple_of((self.starts_ref[self.line + e, b] // 16) * 16, 16)

    def col(self, b, i):
        return self.cols_ref[b * TOKS : (b + 1) * TOKS, i : i + 1]

    def gate(self, e, b):
        return self.col(b, EXPERTS + e)

    def choice(self, e, b):
        return self.col(b, 2 * EXPERTS + e)

    def compact(self, e, makers, outs):
        line = lax.broadcasted_iota(jnp.int32, (SPAN, TOKS), 0).astype(F32)
        for b in range(self.blocks):
            base = self.base(e, b)
            slot = self.rows_ref[self.line + e : self.line + e + 1, b * TOKS : (b + 1) * TOKS] - base.astype(F32)
            hot = jnp.where(slot == line, 1.0, 0.0).astype(BF)
            for make, out in zip(makers, outs):
                rows = mm(hot, make(b)).astype(BF)
                if b == 0:
                    out[pl.ds(base, SPAN), :] = rows
                else:
                    out[pl.ds(base, 16), :] += rows[:16]
                    out[pl.ds(base + 16, TOKS), :] = rows[16:]
        end = self.base(e, self.blocks - 1) + SPAN
        for out in outs:
            out[pl.ds(end, ROWS), :] = jnp.zeros((ROWS, out.shape[1]), BF)

    def spread(self, e, b, ref):
        base = self.base(e, b)
        line = lax.broadcasted_iota(jnp.int32, (TOKS, SPAN), 1).astype(F32)
        hot = jnp.where(self.col(b, e) - base.astype(F32) == line, 1.0, 0.0).astype(BF)
        return mm(hot, ref[pl.ds(base, SPAN), :])

    def zero_after(self, e, ref):
        end = pl.multiple_of(self.tiles(e) * ROWS, ROWS)
        ref[pl.ds(end, SPAN), :] = jnp.zeros((SPAN, ref.shape[1]), BF)


def routing_kernel(t0, t1, t2, t3, rows_ref, cols_a_ref, cols_b_ref, starts_ref):
    tables = (t0, t1, t2, t3)
    tok = t0.shape[1]
    blocks = len(tables) * tok // TOKS
    first = (lax.axis_index("ep") * EXPERTS).astype(F32)
    line = lax.broadcasted_iota(jnp.int32, (8, TOKS), 0)
    target = first + (line % EXPERTS).astype(F32)
    lane = lax.broadcasted_iota(jnp.int32, (8, 128), 1)
    upto = (lax.broadcasted_iota(jnp.int32, (TOKS, TOKS), 0) <= lax.broadcasted_iota(jnp.int32, (TOKS, TOKS), 1)).astype(F32).astype(BF)
    seen = jnp.zeros((8, 1), F32)
    starts = jnp.zeros((8, 128), F32)
    for b in range(blocks):
        at = b * TOKS
        table = tables[at // tok][:, at % tok : at % tok + TOKS]

        def both(i, other):
            return jnp.where(line < EXPERTS, table[i : i + 1], jnp.where(line < 2 * EXPERTS, table[i + 2 : i + 3], other))

        hit0 = both(0, -1.0) == target
        hit1 = both(1, -1.0) == target
        mask = jnp.where(hit0 | hit1, 1.0, 0.0)
        count = mm(mask.astype(BF), upto)
        slot = jnp.where(mask > 0.0, seen + count - 1.0, -1.0)
        gate = jnp.where(hit0, both(4, 0.0), 0.0) + jnp.where(hit1, both(5, 0.0), 0.0)
        choice = jnp.where(hit1, 1.0, 0.0)
        rows_ref[:, at : at + TOKS] = slot
        starts = jnp.where(lane == b, seen, starts)
        for layer, cols_ref in ((0, cols_a_ref), (1, cols_b_ref)):
            part = slice(layer * EXPERTS, (layer + 1) * EXPERTS)
            stack = jnp.concatenate([slot[part], gate[part], choice[part], choice[part]], axis=0)
            cols_ref[at : at + TOKS, :] = stack.T
        seen = seen + count[:, TOKS - 1 :]
    starts_ref[...] = jnp.where(lane == blocks, seen, starts).astype(jnp.int32)


def weight_copies(hbm, vmem, sems, e):
    return [pltpu.make_async_copy(h.at[e], v.at[e], sems.at[e, i]) for i, (h, v) in enumerate(zip(hbm, vmem))]


def forward_kernel(layer, starts_ref, x0, x1, x2, x3, rows_ref, cols_ref, w1_hbm, w3_hbm, w2_hbm,
                   y0, y1, y2, y3, w1, w3, w2, u_all, o_all, h_ref, y_buf, w_sems, y_sems):
    xs, ys = (x0, x1, x2, x3), (y0, y1, y2, y3)
    blocks = rows_ref.shape[1] // TOKS
    width = w1.shape[2]
    slots = Slots(layer, starts_ref, rows_ref, cols_ref, blocks)
    for e in range(EXPERTS):
        for copy in weight_copies((w1_hbm, w3_hbm, w2_hbm), (w1, w3, w2), w_sems, e):
            copy.start()

    def tokens_of(b):
        ref, toks = block_of(xs, b)
        return ref[toks, :]

    for e in range(EXPERTS):
        slots.compact(e, (tokens_of,), (u_all.at[e],))

    def expert(e, carry):
        for copy in weight_copies((w1_hbm, w3_hbm, w2_hbm), (w1, w3, w2), w_sems, e):
            copy.wait()

        def tile(k, inner):
            u = u_all[e, tile_rows(k), :]
            for c in range(0, width, COLS):
                cols = slice(c, c + COLS)
                a = mm(u, w1[e, :, cols])
                b = mm(u, w3[e, :, cols])
                h_ref[:, cols] = (a * jax.nn.sigmoid(a) * b).astype(BF)
            o_all[e, tile_rows(k), :] = mm(h_ref[...], w2[e]).astype(BF)
            return inner

        return lax.fori_loop(0, slots.tiles(e), tile, carry)

    lax.fori_loop(0, EXPERTS, expert, 0)
    for e in range(EXPERTS):
        slots.zero_after(e, o_all.at[e])
    copies = []
    for b in range(blocks):
        y_buf[b] = sum(slots.gate(e, b) * slots.spread(e, b, o_all.at[e]) for e in range(EXPERTS))
        ref, toks = block_of(ys, b)
        copies.append(pltpu.make_async_copy(y_buf.at[b], ref.at[toks, :], y_sems.at[b]))
        copies[-1].start()
    for copy in copies:
        copy.wait()


def dx_kernel(layer, starts_ref, x0, x1, x2, x3, g0, g1, g2, g3, rows_ref, cols_ref, w1_hbm, w3_hbm, w2_hbm,
              dx0, dx1, dx2, dx3, kept_hbm, w1, w3, w2, u_all, q_all, od_all, kept, dx_buf, dg_buf, w_sems, k_sems, dx_sems, dg_sems):
    xs, gs, dxs = (x0, x1, x2, x3), (g0, g1, g2, g3), (dx0, dx1, dx2, dx3)
    tok = x0.shape[0]
    blocks = rows_ref.shape[1] // TOKS
    dim, width = w1.shape[1:]
    slots = Slots(layer, starts_ref, rows_ref, cols_ref, blocks)
    for e in range(EXPERTS):
        for copy in weight_copies((w1_hbm, w3_hbm, w2_hbm), (w1, w3, w2), w_sems, e):
            copy.start()

    def tokens_of(b):
        ref, toks = block_of(xs, b)
        return ref[toks, :]

    for e in range(EXPERTS):

        def scaled_of(b):
            ref, toks = block_of(gs, b)
            return (slots.gate(e, b) * ref[toks, :].astype(F32)).astype(BF)

        slots.compact(e, (tokens_of, scaled_of), (u_all.at[e], q_all.at[e]))

    def copy_out(e, k):
        return pltpu.make_async_copy(kept.at[lax.rem(k, 2)], kept_hbm.at[e, tile_rows(k), :], k_sems.at[lax.rem(k, 2)])

    def expert(e, carry):
        for copy in weight_copies((w1_hbm, w3_hbm, w2_hbm), (w1, w3, w2), w_sems, e):
            copy.wait()
        count = slots.tiles(e)

        def tile(k, inner):
            slot = lax.rem(k, 2)

            @pl.when(k >= 2)
            def _():
                copy_out(e, k - 2).wait()

            u = u_all[e, tile_rows(k), :]
            q = q_all[e, tile_rows(k), :]
            for c in range(0, width, COLS):
                cols = slice(c, c + COLS)
                a = mm(u, w1[e, :, cols])
                b = mm(u, w3[e, :, cols])
                dh = mm_nt(q, w2[e, cols, :])
                s = jax.nn.sigmoid(a)
                act = a * s
                kept[slot, :, c : c + COLS] = (act * b).astype(BF)
                kept[slot, :, width + c : width + c + COLS] = (dh * b * s * (1.0 + a * (1.0 - s))).astype(BF)
                kept[slot, :, 2 * width + c : 2 * width + c + COLS] = (dh * act).astype(BF)
            kept[slot, :, 3 * width : 3 * width + dim] = u
            kept[slot, :, 3 * width + dim :] = q
            od_all[e, tile_rows(k), :dim] = mm(kept[slot, :, :width], w2[e]).astype(BF)
            du = mm_nt(kept[slot, :, width : 2 * width], w1[e]) + mm_nt(kept[slot, :, 2 * width : 3 * width], w3[e])
            od_all[e, tile_rows(k), dim:] = du.astype(BF)
            copy_out(e, k).start()
            return inner

        lax.fori_loop(0, count, tile, 0)

        @pl.when(count >= 2)
        def _():
            copy_out(e, count - 2).wait()

        @pl.when(count >= 1)
        def _():
            copy_out(e, count - 1).wait()

        return carry

    lax.fori_loop(0, EXPERTS, expert, 0)
    for e in range(EXPERTS):
        slots.zero_after(e, od_all.at[e])
    copies = []
    lane = lax.broadcasted_iota(jnp.int32, (TOKS, 8), 1).astype(F32)
    for b in range(blocks):
        gref, toks = block_of(gs, b)
        dy = gref[toks, :].astype(F32)
        dx = jnp.zeros((TOKS, dim), F32)
        dg = jnp.zeros((TOKS, 8), F32)
        for e in range(EXPERTS):
            od = slots.spread(e, b, od_all.at[e])
            dx += od[:, dim:]
            dg += jnp.where(lane == slots.choice(e, b), jnp.sum(dy * od[:, :dim], axis=1, keepdims=True), 0.0)
        dx_buf[b] = dx
        dg_buf[b * TOKS // tok, :, toks] = dg.T
        copies.append(pltpu.make_async_copy(dx_buf.at[b], block_of(dxs, b)[0].at[toks, :], dx_sems.at[b]))
        copies[-1].start()
    for i, dst in enumerate(dxs):
        copies.append(pltpu.make_async_copy(dg_buf.at[i], dst.at[tok : tok + 8, :], dg_sems.at[i]))
        copies[-1].start()
    for copy in copies:
        copy.wait()


def dw_kernel(layer, starts_ref, kept_hbm, dw1_hbm, dw3_hbm, dw2_hbm, kept, dw1, dw3, dw2, k_sems, o_sems):
    dim, width = dw1.shape[1:]
    blocks = kept_hbm.shape[1] // TOKS
    slots = Slots(layer, starts_ref, None, None, blocks)

    def copy_in(e, k, slot):
        return pltpu.make_async_copy(kept_hbm.at[e, tile_rows(k), :], kept.at[slot], k_sems.at[slot])

    def copy_out(e, i):
        return pltpu.make_async_copy((dw1, dw3, dw2)[i].at[e], (dw1_hbm, dw3_hbm, dw2_hbm)[i].at[e], o_sems.at[e, i])

    first_tiles = slots.tiles(0)
    count = first_tiles + slots.tiles(1)

    def where(g):
        e = (g >= first_tiles).astype(jnp.int32)
        return e, g - e * first_tiles

    copy_in(*where(0), 0).start()

    def tile(g, carry):
        slot = lax.rem(g, 2)
        e, k = where(g)
        copy_in(e, k, slot).wait()

        @pl.when(g + 1 < count)
        def _():
            copy_in(*where(g + 1), 1 - slot).start()

        u = kept[slot, :, 3 * width : 3 * width + dim]
        q = kept[slot, :, 3 * width + dim :]
        fresh = k == 0
        last = (g == first_tiles - 1) | (g == count - 1)

        def put(ref, index, part):
            ref[index] = jnp.where(fresh, part, ref[index] + part)

        def leave(i):
            pl.when(last)(lambda: copy_out(e, i).start())

        for c in range(0, width, COLS):
            put(dw1, (e, slice(None), slice(c, c + COLS)), mm_tn(u, kept[slot, :, width + c : width + c + COLS]))
        leave(0)
        for c in range(0, width, COLS):
            put(dw3, (e, slice(None), slice(c, c + COLS)), mm_tn(u, kept[slot, :, 2 * width + c : 2 * width + c + COLS]))
        leave(1)
        for c in range(0, width, COLS):
            put(dw2, (e, slice(c, c + COLS), slice(None)), mm_tn(kept[slot, :, c : c + COLS], q))
        leave(2)
        return carry

    lax.fori_loop(0, count, tile, 0)
    for e in range(EXPERTS):
        for i in range(3):
            copy_out(e, i).wait()


IN_VMEM = pl.BlockSpec(memory_space=pltpu.VMEM)
IN_SMEM = pl.BlockSpec(memory_space=pltpu.SMEM)
IN_HBM = pl.BlockSpec(memory_space=pl.ANY)


def call(kernel, layer, operands, in_specs, outs, out_specs, scratch, flops):
    return pl.pallas_call(
        lambda *refs: kernel(layer, *refs) if layer is not None else kernel(*refs),
        in_specs=in_specs,
        out_specs=out_specs,
        out_shape=outs,
        scratch_shapes=scratch,
        compiler_params=pltpu.CompilerParams(vmem_limit_bytes=VMEM),
        cost_estimate=pl.CostEstimate(flops=flops, bytes_accessed=40_000_000, transcendentals=0),
    )(*operands)


def run_routing(tables):
    tokens = tables[0].shape[1] * len(tables)
    rows, cols_a, cols_b, starts = call(
        routing_kernel, None, tables, [IN_VMEM] * 4,
        [
            jax.ShapeDtypeStruct((8, tokens), F32),
            jax.ShapeDtypeStruct((tokens, 8), F32),
            jax.ShapeDtypeStruct((tokens, 8), F32),
            jax.ShapeDtypeStruct((8, 128), jnp.int32),
        ],
        [IN_VMEM] * 4, [], 10_000_000,
    )
    return (starts, rows, cols_a), (starts, rows, cols_b)


def weight_scratch(w1, w2):
    return [pltpu.VMEM(w1.shape, BF), pltpu.VMEM(w1.shape, BF), pltpu.VMEM(w2.shape, BF)]


def run_forward(layer, xs, maps, w1, w3, w2):
    tok, dim = xs[0].shape
    tokens = tok * len(xs)
    width = w1.shape[2]
    blocks = tokens // TOKS
    most = tokens + SPAN + ROWS
    return call(
        forward_kernel, layer, (maps[0], *xs, maps[1], maps[2], w1, w3, w2),
        [IN_SMEM] + [IN_VMEM] * 6 + [IN_HBM] * 3,
        [jax.ShapeDtypeStruct((tok, dim), F32)] * 4,
        [IN_HBM] * 4,
        weight_scratch(w1, w2)
        + [pltpu.VMEM((EXPERTS, most, dim), BF)] * 2
        + [pltpu.VMEM((ROWS, width), BF), pltpu.VMEM((blocks, TOKS, dim), F32)]
        + [pltpu.SemaphoreType.DMA((EXPERTS, 3)), pltpu.SemaphoreType.DMA((blocks,))],
        2 * 3 * tokens * dim * width,
    )


def run_dx(layer, xs, gs, maps, w1, w3, w2):
    tok, dim = xs[0].shape
    tokens = tok * len(xs)
    width = w1.shape[2]
    blocks = tokens // TOKS
    most = tokens + SPAN + ROWS
    kept = 3 * width + 2 * dim
    out = call(
        dx_kernel, layer, (maps[0], *xs, *gs, maps[1], maps[2], w1, w3, w2),
        [IN_SMEM] + [IN_VMEM] * 10 + [IN_HBM] * 3,
        [jax.ShapeDtypeStruct((tok + 8, dim), F32)] * 4 + [jax.ShapeDtypeStruct((EXPERTS, tokens, kept), BF)],
        [IN_HBM] * 5,
        weight_scratch(w1, w2)
        + [pltpu.VMEM((EXPERTS, most, dim), BF)] * 2
        + [pltpu.VMEM((EXPERTS, most, 2 * dim), BF), pltpu.VMEM((2, ROWS, kept), BF), pltpu.VMEM((blocks, TOKS, dim), F32)]
        + [pltpu.VMEM((4, 8, tok), F32)]
        + [pltpu.SemaphoreType.DMA((EXPERTS, 3)), pltpu.SemaphoreType.DMA((2,)), pltpu.SemaphoreType.DMA((blocks,))]
        + [pltpu.SemaphoreType.DMA((4,))],
        2 * 6 * tokens * dim * width,
    )
    return out[:4], out[4]


def run_dw(layer, kept, maps, shape1, shape2):
    tokens = kept.shape[1]
    return call(
        dw_kernel, layer, (maps[0], kept),
        [IN_SMEM, IN_HBM],
        [jax.ShapeDtypeStruct(shape1, F32), jax.ShapeDtypeStruct(shape1, F32), jax.ShapeDtypeStruct(shape2, F32)],
        [IN_HBM] * 3,
        [pltpu.VMEM((2, ROWS, kept.shape[2]), BF), pltpu.VMEM(shape1, F32), pltpu.VMEM(shape1, F32), pltpu.VMEM(shape2, F32)]
        + [pltpu.SemaphoreType.DMA((2,)), pltpu.SemaphoreType.DMA((EXPERTS, 3))],
        2 * 3 * tokens * shape1[1] * shape1[2],
    )


def solution(mesh):
    tok_spec = P(("dp", "ep"))
    w_spec = P("ep")
    across = [(0, 2), (2, 0), (1, 3), (3, 1)]
    beside = [(0, 1), (1, 0), (2, 3), (3, 2)]
    cross = [(0, 3), (3, 0), (1, 2), (2, 1)]

    def permute(v, pairs):
        return lax.ppermute(v, "ep", pairs)

    def gather(own):
        other = permute(own, across)
        return other, permute(other, beside), own, permute(own, beside)

    def gather_direct(own):
        return permute(own, across), permute(own, cross), own, permute(own, beside)

    def combine(parts):
        other, diagonal, own, mate = parts
        theirs = other + permute(diagonal, beside)
        return own + permute(mate, beside) + permute(theirs, across)

    def device_program(x_in, idx_a, idx_b, gate_a, gate_b, dy_out, w1_a, w3_a, w2_a, w1_b, w3_b, w2_b):
        tok, top_k = idx_a.shape
        own_map = jnp.concatenate([idx_a.astype(F32), idx_b.astype(F32), gate_a, gate_b], axis=1).T
        maps_a, maps_b = run_routing(gather_direct(own_map))

        def add(base, total):
            return (base.astype(F32) + total[:tok]).astype(BF)

        def dgate_of(total):
            return total[tok : tok + top_k].T

        x_all = gather(x_in)
        dy_all = gather_direct(dy_out)
        x_mid = add(x_in, combine(run_forward(0, x_all, maps_a, w1_a, w3_a, w2_a)))
        mid_all = gather(x_mid)
        x_again, mid_other = lax.optimization_barrier((x_in, mid_all[0]))
        mid_all = (mid_other, *mid_all[1:])
        again_all = gather_direct(x_again)
        dx_parts, kept_b = run_dx(1, mid_all, dy_all, maps_b, w1_b, w3_b, w2_b)
        total = combine(dx_parts)
        dx_mid, dgate_b = add(dy_out, total), dgate_of(total)
        dmid_all = gather_direct(dx_mid)
        x_out = add(x_mid, combine(run_forward(1, mid_all, maps_b, w1_b, w3_b, w2_b)))
        grads_b = run_dw(1, kept_b, maps_b, w1_b.shape, w2_b.shape)
        dx_parts, kept_a = run_dx(0, again_all, dmid_all, maps_a, w1_a, w3_a, w2_a)
        total = combine(dx_parts)
        dx_in, dgate_a = add(dx_mid, total), dgate_of(total)
        grads_a = run_dw(0, kept_a, maps_a, w1_a.shape, w2_a.shape)
        return (x_out, dx_in, *grads_a, *grads_b, dgate_a, dgate_b)


    return jax.shard_map(device_program, mesh=mesh, in_specs=(tok_spec,) * 6 + (w_spec,) * 6, out_specs=(tok_spec,) * 10, check_vma=False)
```

time: 1030 us -> 359 us (0.35)
  matrix products: 407 us -> 0 us
  local copies, waits for them, and re-layouts: 300 us -> 5.27 us
  Pallas kernels: 0 us -> 121 us
  blocking collectives: 104 us -> 0 us
  starting transfers between devices: 49.8 us -> 87 us
  other arithmetic: 45.9 us -> 19 us
    dot_general x24 -> x0, matrix products: 407 us -> none  [the longest x4 81.1 us: expert_forward(): jnp.einsum('erd,edf->erf', u_rows, w_up, preferred_element_type=jnp.float32)]
    gather x13 -> x0, local copies, waits for them, and re-layouts: 163 us -> none  [the longest x7 120 us: send_rows(): send_buf = jnp.take(rows, index, axis=0, mode='fill', fill_value=0)]
    pallas_call x0 -> x7, Pallas kernels: none -> 121 us  [call(): pl.pallas_call(lambda *refs: kernel(layer, *refs) if layer is not None el...]
    ppermute x0 -> x30, waiting for transfers between devices: none -> 120 us  [permute(): return lax.ppermute(v, 'ep', pairs)]
    all_to_all x11 -> x0, waiting for transfers between devices: 116 us -> none  [the longest x6 59.5 us: send_back(): back_rows = lax.all_to_all(rows, 'ep', 1, 0, tiled=True)]
    all_to_all x2 -> x0, blocking collectives: 104 us -> none  [send_rows(): return lax.all_to_all(send_buf, 'ep', 0, 1, tiled=True)]
    ppermute x0 -> x30, starting transfers between devices: none -> 87 us  [permute(): return lax.ppermute(v, 'ep', pairs)]
    convert_element_type x8 -> x0, local copies, waits for them, and re-layouts: 67.4 us -> none  [the longest x2 38.1 us: expert_backward(): (jnp.einsum('erf,edf->erd', d_pre_gate, w_gate, preferred_element_type=jn...]
  transfers between devices with their start and end apart: 11 -> 30, of which waited for: 7 -> 14; matrix products, arithmetic and copies ran while one was open for 36% -> 5% of each run, Pallas kernels for 0% -> 22%
where the time goes in v2:
time: 359 us; the launch traced here: 354 us
  Pallas kernels  121 us (34%)
  waiting for transfers between devices  120 us (33%)
  starting transfers between devices  87 us (24%)
  other arithmetic  19 us (5%)
  local copies, waits for them, and re-layouts  5.27 us (1%)
    pallas_call x7, Pallas kernels, call(): pl.pallas_call(lambda *refs: kernel(layer, *refs) if layer is not None el...  121 us
    ppermute x30, waiting for transfers between devices, permute(): return lax.ppermute(v, 'ep', pairs)  120 us
    ppermute x30, starting transfers between devices, permute(): return lax.ppermute(v, 'ep', pairs)  87 us
    add x4, other arithmetic, combine(): theirs = other + permute(diagonal, beside)  7.63 us
  transfers between devices with their start and end apart: 30, of which 14 were waited for; matrix products, arithmetic and copies ran while one was open for 5% of the time, Pallas kernels for 22%

profile of v2, /device:TPU:0, one launch (start us, length us, event | category | flops | bytes accessed | tf_op | source)
XLA Modules:
  0.0 353.8 jit_solution(17197705906284418949)
XLA Ops:
  0.6 3.3 collective-permute-start.3
  4.0 12.1 %collective-permute-done.3.refs_1_ = bf16[512,512]{1,0:T(8,128)(2,1)S(1)} collective-permute-done((bf16[512,512]{1,0:T(8,128)(2,1)}, bf16[512,512]{1,0:T(8,128)(2,1)S(1)}, u32[]{:S(2)}, u32[]{:S(2)}) %collective-permute-start.3) | collective-permute-done | bytes 524320 | tf_op jit(solution)/shard_map/ppermute | solution.py:425
  21.9 1.9 collective-permute-done.refs_0_
  24.5 2.9 shard_map.195
  27.4 15.5 %shard_map.196 = (f32[512,512]{1,0:T(8,128)}, f32[512,512]{1,0:T(8,128)}, f32[512,512]{1,0:T(8,128)}, f32[512,512]{1,0:T(8,128)}) custom-call(s32[8,128]{1,0:T(8,128)} %get-tuple-element.40.refs_0_, bf16[512,512]{1,0:T(8,128)(2,1)} %copy-done.21, bf16[512,512]{1,0:T(8,128)(2,1)} %collective-permute-done.4.refs_2_, bf16[512,512]{1,0:T(8,128)(2,1)} %refs_3_.2, ...), custom_call_target="tpu_custom_call" | custom-call | flops 11274289152 | bytes 40000000 | tf_op jit(solution)/shard_map/pallas_call | solution.py:332
  43.4 2.4 collective-permute-done.7
  47.4 10.0 %collective-permute-start.8 = (f32[512,512]{1,0:T(8,128)S(1)}, f32[512,512]{1,0:T(8,128)S(1)}, u32[]{:S(2)}, u32[]{:S(2)}) collective-permute-start(f32[512,512]{1,0:T(8,128)S(1)} %add.49), channel_id=1, source_target_pairs={{0,2},{2,0},{1,3},{3,1},{4,6},{6,4},{5,7},{7,5}} | collective-permute-start | bytes 3145736 | tf_op jit(solution)/shard_map/ppermute | solution.py:425
  57.3 23.5 %collective-permute-done.8 = f32[512,512]{1,0:T(8,128)S(1)} collective-permute-done((f32[512,512]{1,0:T(8,128)S(1)}, f32[512,512]{1,0:T(8,128)S(1)}, u32[]{:S(2)}, u32[]{:S(2)}) %collective-permute-start.8) | collective-permute-done | bytes 1048608 | tf_op jit(solution)/shard_map/ppermute | solution.py:425
  81.2 1.8 collective-permute-start.9
  84.9 11.2 %collective-permute-done.9.refs_1_ = bf16[512,512]{1,0:T(8,128)(2,1)S(1)} collective-permute-done((bf16[512,512]{1,0:T(8,128)(2,1)S(1)}, bf16[512,512]{1,0:T(8,128)(2,1)S(1)}, u32[]{:S(2)}, u32[]{:S(2)}) %collective-permute-start.9) | collective-permute-done | bytes 524320 | tf_op jit(solution)/shard_map/ppermute | solution.py:425
  96.1 10.5 %collective-permute-done.16.refs_6_ = bf16[512,512]{1,0:T(8,128)(2,1)S(1)} collective-permute-done((bf16[512,512]{1,0:T(8,128)(2,1)S(1)}, bf16[512,512]{1,0:T(8,128)(2,1)S(1)}, u32[]{:S(2)}, u32[]{:S(2)}) %collective-permute-start.16) | collective-permute-done | bytes 524320 | tf_op jit(solution)/shard_map/ppermute | solution.py:425
  106.5 10.6 %collective-permute-done.15.refs_5_ = bf16[512,512]{1,0:T(8,128)(2,1)S(1)} collective-permute-done((bf16[512,512]{1,0:T(8,128)(2,1)S(1)}, bf16[512,512]{1,0:T(8,128)(2,1)S(1)}, u32[]{:S(2)}, u32[]{:S(2)}) %collective-permute-start.15) | collective-permute-done | bytes 524320 | tf_op jit(solution)/shard_map/ppermute | solution.py:425
  119.1 27.0 %shard_map.198 = (f32[520,512]{1,0:T(8,128)}, f32[520,512]{1,0:T(8,128)}, f32[520,512]{1,0:T(8,128)}, f32[520,512]{1,0:T(8,128)}, bf16[2,2048,6400]{2,1,0:T(8,128)(2,1)}) custom-call(s32[8,128]{1,0:T(8,128)} %get-tuple-element.40.refs_0_, bf16[512,512]{1,0:T(8,128)(2,1)} %copy-done.17, bf16[512,512]{1,0:T(8,128)(2,1)} %copy-done.22, ...), custom_call_target="tpu_custom_call" | custom-call | flops 22548578304 | bytes 40000000 | tf_op jit(solution)/shard_map/pallas_call | solution.py:332
  146.6 2.4 collective-permute-done.19
  149.0 2.4 add.57
  151.4 20.1 %collective-permute-start.20 = (f32[520,512]{1,0:T(8,128)}, f32[520,512]{1,0:T(8,128)}, u32[]{:S(2)}, u32[]{:S(2)}) collective-permute-start(f32[520,512]{1,0:T(8,128)} %add.57), channel_id=1, source_target_pairs={{0,2},{2,0},{1,3},{3,1},{4,6},{6,4},{5,7},{7,5}} | collective-permute-start | bytes 3194888 | tf_op jit(solution)/shard_map/ppermute | solution.py:425
  171.6 15.6 %shard_map.197 = (f32[512,512]{1,0:T(8,128)}, f32[512,512]{1,0:T(8,128)}, f32[512,512]{1,0:T(8,128)}, f32[512,512]{1,0:T(8,128)}) custom-call(s32[8,128]{1,0:T(8,128)} %get-tuple-element.40.refs_0_, bf16[512,512]{1,0:T(8,128)(2,1)} %copy-done.17, bf16[512,512]{1,0:T(8,128)(2,1)} %copy-done.22, bf16[512,512]{1,0:T(8,128)(2,1)} %copy-done.3, ...), custom_call_target="tpu_custom_call" | custom-call | flops 11274289152 | bytes 40000000 | tf_op jit(solution)/shard_map/pallas_call | solution.py:332
  187.8 9.3 %collective-permute-start.22 = (bf16[512,512]{1,0:T(8,128)(2,1)S(1)}, bf16[512,512]{1,0:T(8,128)(2,1)S(1)}, u32[]{:S(2)}, u32[]{:S(2)}) collective-permute-start(bf16[512,512]{1,0:T(8,128)(2,1)S(1)} %copy-done.11), channel_id=1, source_target_pairs={{0,3},{3,0},{1,2},{2,1},{4,7},{7,4},{5,6},{6,5}} | collective-permute-start | bytes 1572872 | tf_op jit(solution)/shard_map/ppermute | solution.py:425
  197.4 2.3 add_add_fusion.1
  203.3 6.0 %collective-permute-done.22.refs_2_ = bf16[512,512]{1,0:T(8,128)(2,1)S(1)} collective-permute-done((bf16[512,512]{1,0:T(8,128)(2,1)S(1)}, bf16[512,512]{1,0:T(8,128)(2,1)S(1)}, u32[]{:S(2)}, u32[]{:S(2)}) %collective-permute-start.22) | collective-permute-done | bytes 524320 | tf_op jit(solution)/shard_map/ppermute | solution.py:425
  210.0 11.4 %collective-permute-done.21.refs_1_ = bf16[512,512]{1,0:T(8,128)(2,1)S(1)} collective-permute-done((bf16[512,512]{1,0:T(8,128)(2,1)S(1)}, bf16[512,512]{1,0:T(8,128)(2,1)S(1)}, u32[]{:S(2)}, u32[]{:S(2)}) %collective-permute-start.21) | collective-permute-done | bytes 524320 | tf_op jit(solution)/shard_map/ppermute | solution.py:425
  221.4 1.7 collective-permute-start.14
  223.1 8.7 %collective-permute-done.25.refs_6_ = bf16[512,512]{1,0:T(8,128)(2,1)S(1)} collective-permute-done((bf16[512,512]{1,0:T(8,128)(2,1)S(1)}, bf16[512,512]{1,0:T(8,128)(2,1)S(1)}, u32[]{:S(2)}, u32[]{:S(2)}) %collective-permute-start.25) | collective-permute-done | bytes 524320 | tf_op jit(solution)/shard_map/ppermute | solution.py:425
  232.6 11.3 %collective-permute-done.24.refs_5_ = bf16[512,512]{1,0:T(8,128)(2,1)} collective-permute-done((bf16[512,512]{1,0:T(8,128)(2,1)S(1)}, bf16[512,512]{1,0:T(8,128)(2,1)}, u32[]{:S(2)}, u32[]{:S(2)}) %collective-permute-start.24) | collective-permute-done | bytes 524320 | tf_op jit(solution)/shard_map/ppermute | solution.py:425
  244.0 26.9 %shard_map.199 = (f32[520,512]{1,0:T(8,128)}, f32[520,512]{1,0:T(8,128)}, f32[520,512]{1,0:T(8,128)}, f32[520,512]{1,0:T(8,128)}, bf16[2,2048,6400]{2,1,0:T(8,128)(2,1)}) custom-call(s32[8,128]{1,0:T(8,128)} %get-tuple-element.40.refs_0_, bf16[512,512]{1,0:T(8,128)(2,1)} %copy-done.19, bf16[512,512]{1,0:T(8,128)(2,1)} %copy-done.18, ...), custom_call_target="tpu_custom_call" | custom-call | flops 22548578304 | bytes 40000000 | tf_op jit(solution)/shard_map/pallas_call | solution.py:332
  270.9 16.7 %shard_map.201 = (f32[2,512,1792]{2,1,0:T(8,128)}, f32[2,512,1792]{2,1,0:T(8,128)}, f32[2,1792,512]{2,1,0:T(8,128)}) custom-call(s32[8,128]{1,0:T(8,128)} %get-tuple-element.40.refs_0_, bf16[2,2048,6400]{2,1,0:T(8,128)(2,1)} %get-tuple-element.66.refs_1_), custom_call_target="tpu_custom_call" | custom-call | flops 11274289152 | bytes 40000000 | tf_op jit(solution)/shard_map/pallas_call | solution.py:332
  287.7 3.2 add_convert_fusion
  291.3 2.4 add.61
  293.8 31.4 %collective-permute-start.29 = (f32[520,512]{1,0:T(8,128)}, f32[520,512]{1,0:T(8,128)}, u32[]{:S(2)}, u32[]{:S(2)}) collective-permute-start(f32[520,512]{1,0:T(8,128)} %add.61), channel_id=1, source_target_pairs={{0,2},{2,0},{1,3},{3,1},{4,6},{6,4},{5,7},{7,5}} | collective-permute-start | bytes 3194888 | tf_op jit(solution)/shard_map/ppermute | solution.py:425
  326.5 16.6 %shard_map.200 = (f32[2,512,1792]{2,1,0:T(8,128)}, f32[2,512,1792]{2,1,0:T(8,128)}, f32[2,1792,512]{2,1,0:T(8,128)}) custom-call(s32[8,128]{1,0:T(8,128)} %get-tuple-element.40.refs_0_, bf16[2,2048,6400]{2,1,0:T(8,128)(2,1)} %get-tuple-element.62.refs_1_), custom_call_target="tpu_custom_call" | custom-call | flops 11274289152 | bytes 40000000 | tf_op jit(solution)/shard_map/pallas_call | solution.py:332
  343.1 6.6 %collective-permute-done.29 = f32[520,512]{1,0:T(8,128)} collective-permute-done((f32[520,512]{1,0:T(8,128)}, f32[520,512]{1,0:T(8,128)}, u32[]{:S(2)}, u32[]{:S(2)}) %collective-permute-start.29) | collective-permute-done | bytes 1064992 | tf_op jit(solution)/shard_map/ppermute | solution.py:425
  349.7 2.3 add_add_fusion
  (106 shorter events, 22.5 us)
Async XLA Ops:
  0.6 15.5 %collective-permute-start.3 = (bf16[512,512]{1,0:T(8,128)(2,1)}, bf16[512,512]{1,0:T(8,128)(2,1)S(1)}, u32[]{:S(2)}, u32[]{:S(2)}) collective-permute-start(bf16[512,512]{1,0:T(8,128)(2,1)} %refs_3_.2), channel_id=1, source_target_pairs={{0,2},{2,0},{1,3},{3,1},{4,6},{6,4},{5,7},{7,5}} | collective-permute-start | bytes 1572872 | tf_op jit(solution)/shard_map/ppermute | solution.py:425
  4.0 23.4 %collective-permute-start.5 = (bf16[512,512]{1,0:T(8,128)(2,1)}, bf16[512,512]{1,0:T(8,128)(2,1)}, u32[]{:S(2)}, u32[]{:S(2)}) collective-permute-start(bf16[512,512]{1,0:T(8,128)(2,1)} %refs_3_.2), channel_id=1, source_target_pairs={{0,1},{1,0},{2,3},{3,2},{4,5},{5,4},{6,7},{7,6}} | collective-permute-start | bytes 1572872 | tf_op jit(solution)/shard_map/ppermute | solution.py:425
  16.1 11.3 %collective-permute-start.4 = (bf16[512,512]{1,0:T(8,128)(2,1)S(1)}, bf16[512,512]{1,0:T(8,128)(2,1)}, u32[]{:S(2)}, u32[]{:S(2)}) collective-permute-start(bf16[512,512]{1,0:T(8,128)(2,1)S(1)} %collective-permute-done.3.refs_1_), channel_id=1, source_target_pairs={{0,1},{1,0},{2,3},{3,2},{4,5},{5,4},{6,7},{7,6}} | collective-permute-start | bytes 1572872 | tf_op jit(solution)/shard_map/ppermute | solution.py:425
  18.2 2.3 collective-permute-start.2
  18.8 3.2 collective-permute-start.1
  20.1 3.7 %collective-permute-start = (f32[8,512]{1,0:T(8,128)S(1)}, f32[8,512]{1,0:T(8,128)S(1)}, u32[]{:S(2)}, u32[]{:S(2)}) collective-permute-start(f32[8,512]{1,0:T(8,128)S(1)} %maximum_bitcast_fusion.refs_2_), channel_id=1, source_target_pairs={{0,2},{2,0},{1,3},{3,1},{4,6},{6,4},{5,7},{7,5}} | collective-permute-start | bytes 49160 | tf_op jit(solution)/shard_map/ppermute | solution.py:425
  42.9 2.9 collective-permute-start.7
  42.9 14.4 %collective-permute-start.6 = (f32[512,512]{1,0:T(8,128)}, f32[512,512]{1,0:T(8,128)S(1)}, u32[]{:S(2)}, u32[]{:S(2)}) collective-permute-start(f32[512,512]{1,0:T(8,128)} %get-tuple-element.44), channel_id=1, source_target_pairs={{0,1},{1,0},{2,3},{3,2},{4,5},{5,4},{6,7},{7,6}} | collective-permute-start | bytes 3145736 | tf_op jit(solution)/shard_map/ppermute | solution.py:425
  47.4 33.4 %collective-permute-start.8 = (f32[512,512]{1,0:T(8,128)S(1)}, f32[512,512]{1,0:T(8,128)S(1)}, u32[]{:S(2)}, u32[]{:S(2)}) collective-permute-start(f32[512,512]{1,0:T(8,128)S(1)} %add.49), channel_id=1, source_target_pairs={{0,2},{2,0},{1,3},{3,1},{4,6},{6,4},{5,7},{7,5}} | collective-permute-start | bytes 3145736 | tf_op jit(solution)/shard_map/ppermute | solution.py:425
  81.2 37.8 %copy-start.3 = (bf16[512,512]{1,0:T(8,128)(2,1)}, bf16[512,512]{1,0:T(8,128)(2,1)S(1)}, u32[]{:S(2)}) copy-start(bf16[512,512]{1,0:T(8,128)(2,1)S(1)} %add_convert_fusion.1.refs_3_) | copy-start | bytes 1572868
  81.2 14.8 %collective-permute-start.9 = (bf16[512,512]{1,0:T(8,128)(2,1)S(1)}, bf16[512,512]{1,0:T(8,128)(2,1)S(1)}, u32[]{:S(2)}, u32[]{:S(2)}) collective-permute-start(bf16[512,512]{1,0:T(8,128)(2,1)S(1)} %add_convert_fusion.1.refs_3_), channel_id=1, source_target_pairs={{0,2},{2,0},{1,3},{3,1},{4,6},{6,4},{5,7},{7,5}} | collective-permute-start | bytes 1572872 | tf_op jit(solution)/shard_map/ppermute | solution.py:425
  83.0 23.5 %collective-permute-start.16 = (bf16[512,512]{1,0:T(8,128)(2,1)S(1)}, bf16[512,512]{1,0:T(8,128)(2,1)S(1)}, u32[]{:S(2)}, u32[]{:S(2)}) collective-permute-start(bf16[512,512]{1,0:T(8,128)(2,1)S(1)} %copy-done.8), channel_id=1, source_target_pairs={{0,3},{3,0},{1,2},{2,1},{4,7},{7,4},{5,6},{6,5}} | collective-permute-start | bytes 1572872 | tf_op jit(solution)/shard_map/ppermute | solution.py:425
  83.0 34.1 %collective-permute-start.15 = (bf16[512,512]{1,0:T(8,128)(2,1)S(1)}, bf16[512,512]{1,0:T(8,128)(2,1)S(1)}, u32[]{:S(2)}, u32[]{:S(2)}) collective-permute-start(bf16[512,512]{1,0:T(8,128)(2,1)S(1)} %copy-done.8), channel_id=1, source_target_pairs={{0,2},{2,0},{1,3},{3,1},{4,6},{6,4},{5,7},{7,5}} | collective-permute-start | bytes 1572872 | tf_op jit(solution)/shard_map/ppermute | solution.py:425
  83.6 33.5 %collective-permute-start.17 = (bf16[512,512]{1,0:T(8,128)(2,1)S(1)}, bf16[512,512]{1,0:T(8,128)(2,1)S(1)}, u32[]{:S(2)}, u32[]{:S(2)}) collective-permute-start(bf16[512,512]{1,0:T(8,128)(2,1)S(1)} %copy-done.8), channel_id=1, source_target_pairs={{0,1},{1,0},{2,3},{3,2},{4,5},{5,4},{6,7},{7,6}} | collective-permute-start | bytes 1572872 | tf_op jit(solution)/shard_map/ppermute | solution.py:425
  84.9 32.3 %collective-permute-start.11 = (bf16[512,512]{1,0:T(8,128)(2,1)S(1)}, bf16[512,512]{1,0:T(8,128)(2,1)S(1)}, u32[]{:S(2)}, u32[]{:S(2)}) collective-permute-start(bf16[512,512]{1,0:T(8,128)(2,1)S(1)} %add_convert_fusion.1.refs_3_), channel_id=1, source_target_pairs={{0,1},{1,0},{2,3},{3,2},{4,5},{5,4},{6,7},{7,6}} | collective-permute-start | bytes 1572872 | tf_op jit(solution)/shard_map/ppermute | solution.py:425
  96.1 21.1 %collective-permute-start.10 = (bf16[512,512]{1,0:T(8,128)(2,1)S(1)}, bf16[512,512]{1,0:T(8,128)(2,1)S(1)}, u32[]{:S(2)}, u32[]{:S(2)}) collective-permute-start(bf16[512,512]{1,0:T(8,128)(2,1)S(1)} %collective-permute-done.9.refs_1_), channel_id=1, source_target_pairs={{0,1},{1,0},{2,3},{3,2},{4,5},{5,4},{6,7},{7,6}} | collective-permute-start | bytes 1572872 | tf_op jit(solution)/shard_map/ppermute | solution.py:425
  146.1 2.9 collective-permute-start.19
  146.1 50.9 %collective-permute-start.18 = (f32[520,512]{1,0:T(8,128)}, f32[520,512]{1,0:T(8,128)}, u32[]{:S(2)}, u32[]{:S(2)}) collective-permute-start(f32[520,512]{1,0:T(8,128)} %get-tuple-element.54), channel_id=1, source_target_pairs={{0,1},{1,0},{2,3},{3,2},{4,5},{5,4},{6,7},{7,6}} | collective-permute-start | bytes 3194888 | tf_op jit(solution)/shard_map/ppermute | solution.py:425
  151.4 35.8 %copy-start.11 = (bf16[512,512]{1,0:T(8,128)(2,1)S(1)}, bf16[512,512]{1,0:T(8,128)(2,1)}, u32[]{:S(2)}) copy-start(bf16[512,512]{1,0:T(8,128)(2,1)} %refs_3_.2) | copy-start | bytes 1572868
  151.4 46.0 %collective-permute-start.20 = (f32[520,512]{1,0:T(8,128)}, f32[520,512]{1,0:T(8,128)}, u32[]{:S(2)}, u32[]{:S(2)}) collective-permute-start(f32[520,512]{1,0:T(8,128)} %add.57), channel_id=1, source_target_pairs={{0,2},{2,0},{1,3},{3,1},{4,6},{6,4},{5,7},{7,5}} | collective-permute-start | bytes 3194888 | tf_op jit(solution)/shard_map/ppermute | solution.py:425
  187.2 14.5 %collective-permute-start.13 = (f32[512,512]{1,0:T(8,128)}, f32[512,512]{1,0:T(8,128)S(1)}, u32[]{:S(2)}, u32[]{:S(2)}) collective-permute-start(f32[512,512]{1,0:T(8,128)} %get-tuple-element.52), channel_id=1, source_target_pairs={{0,1},{1,0},{2,3},{3,2},{4,5},{5,4},{6,7},{7,6}} | collective-permute-start | bytes 3145736 | tf_op jit(solution)/shard_map/ppermute | solution.py:425
  187.3 12.8 %collective-permute-start.23 = (bf16[512,512]{1,0:T(8,128)(2,1)S(1)}, bf16[512,512]{1,0:T(8,128)(2,1)S(1)}, u32[]{:S(2)}, u32[]{:S(2)}) collective-permute-start(bf16[512,512]{1,0:T(8,128)(2,1)S(1)} %copy-done.11), channel_id=1, source_target_pairs={{0,1},{1,0},{2,3},{3,2},{4,5},{5,4},{6,7},{7,6}} | collective-permute-start | bytes 1572872 | tf_op jit(solution)/shard_map/ppermute | solution.py:425
  187.8 21.6 %collective-permute-start.22 = (bf16[512,512]{1,0:T(8,128)(2,1)S(1)}, bf16[512,512]{1,0:T(8,128)(2,1)S(1)}, u32[]{:S(2)}, u32[]{:S(2)}) collective-permute-start(bf16[512,512]{1,0:T(8,128)(2,1)S(1)} %copy-done.11), channel_id=1, source_target_pairs={{0,3},{3,0},{1,2},{2,1},{4,7},{7,4},{5,6},{6,5}} | collective-permute-start | bytes 1572872 | tf_op jit(solution)/shard_map/ppermute | solution.py:425
  197.0 24.4 %collective-permute-start.21 = (bf16[512,512]{1,0:T(8,128)(2,1)S(1)}, bf16[512,512]{1,0:T(8,128)(2,1)S(1)}, u32[]{:S(2)}, u32[]{:S(2)}) collective-permute-start(bf16[512,512]{1,0:T(8,128)(2,1)S(1)} %copy-done.11), channel_id=1, source_target_pairs={{0,2},{2,0},{1,3},{3,1},{4,6},{6,4},{5,7},{7,5}} | collective-permute-start | bytes 1572872 | tf_op jit(solution)/shard_map/ppermute | solution.py:425
  199.9 23.2 %collective-permute-start.26 = (bf16[512,512]{1,0:T(8,128)(2,1)S(1)}, bf16[512,512]{1,0:T(8,128)(2,1)S(1)}, u32[]{:S(2)}, u32[]{:S(2)}) collective-permute-start(bf16[512,512]{1,0:T(8,128)(2,1)S(1)} %fusion.1.refs_7_), channel_id=1, source_target_pairs={{0,1},{1,0},{2,3},{3,2},{4,5},{5,4},{6,7},{7,6}} | collective-permute-start | bytes 1572872 | tf_op jit(solution)/shard_map/ppermute | solution.py:425
  200.1 31.8 %collective-permute-start.25 = (bf16[512,512]{1,0:T(8,128)(2,1)S(1)}, bf16[512,512]{1,0:T(8,128)(2,1)S(1)}, u32[]{:S(2)}, u32[]{:S(2)}) collective-permute-start(bf16[512,512]{1,0:T(8,128)(2,1)S(1)} %fusion.1.refs_7_), channel_id=1, source_target_pairs={{0,3},{3,0},{1,2},{2,1},{4,7},{7,4},{5,6},{6,5}} | collective-permute-start | bytes 1572872 | tf_op jit(solution)/shard_map/ppermute | solution.py:425
  201.7 42.3 %collective-permute-start.24 = (bf16[512,512]{1,0:T(8,128)(2,1)S(1)}, bf16[512,512]{1,0:T(8,128)(2,1)}, u32[]{:S(2)}, u32[]{:S(2)}) collective-permute-start(bf16[512,512]{1,0:T(8,128)(2,1)S(1)} %fusion.1.refs_7_), channel_id=1, source_target_pairs={{0,2},{2,0},{1,3},{3,1},{4,6},{6,4},{5,7},{7,5}} | collective-permute-start | bytes 1572872 | tf_op jit(solution)/shard_map/ppermute | solution.py:425
  209.4 78.3 %collective-permute-start.12 = (f32[512,512]{1,0:T(8,128)}, f32[512,512]{1,0:T(8,128)}, u32[]{:S(2)}, u32[]{:S(2)}) collective-permute-start(f32[512,512]{1,0:T(8,128)} %get-tuple-element.50), channel_id=1, source_target_pairs={{0,1},{1,0},{2,3},{3,2},{4,5},{5,4},{6,7},{7,6}} | collective-permute-start | bytes 3145736 | tf_op jit(solution)/shard_map/ppermute | solution.py:425
  221.4 66.3 %collective-permute-start.14 = (f32[512,512]{1,0:T(8,128)}, f32[512,512]{1,0:T(8,128)}, u32[]{:S(2)}, u32[]{:S(2)}) collective-permute-start(f32[512,512]{1,0:T(8,128)} %add.53), channel_id=1, source_target_pairs={{0,2},{2,0},{1,3},{3,1},{4,6},{6,4},{5,7},{7,5}} | collective-permute-start | bytes 3145736 | tf_op jit(solution)/shard_map/ppermute | solution.py:425
  270.9 20.5 %collective-permute-start.28 = (f32[520,512]{1,0:T(8,128)}, f32[520,512]{1,0:T(8,128)}, u32[]{:S(2)}, u32[]{:S(2)}) collective-permute-start(f32[520,512]{1,0:T(8,128)} %get-tuple-element.61), channel_id=1, source_target_pairs={{0,1},{1,0},{2,3},{3,2},{4,5},{5,4},{6,7},{7,6}} | collective-permute-start | bytes 3194888 | tf_op jit(solution)/shard_map/ppermute | solution.py:425
  290.8 52.3 %collective-permute-start.27 = (f32[520,512]{1,0:T(8,128)}, f32[520,512]{1,0:T(8,128)}, u32[]{:S(2)}, u32[]{:S(2)}) collective-permute-start(f32[520,512]{1,0:T(8,128)} %get-tuple-element.59), channel_id=1, source_target_pairs={{0,1},{1,0},{2,3},{3,2},{4,5},{5,4},{6,7},{7,6}} | collective-permute-start | bytes 3194888 | tf_op jit(solution)/shard_map/ppermute | solution.py:425
  293.8 55.9 %collective-permute-start.29 = (f32[520,512]{1,0:T(8,128)}, f32[520,512]{1,0:T(8,128)}, u32[]{:S(2)}, u32[]{:S(2)}) collective-permute-start(f32[520,512]{1,0:T(8,128)} %add.61), channel_id=1, source_target_pairs={{0,2},{2,0},{1,3},{3,1},{4,6},{6,4},{5,7},{7,5}} | collective-permute-start | bytes 3194888 | tf_op jit(solution)/shard_map/ppermute | solution.py:425
  (26 other events, 210.7 us)

commit v3 on v2

v3 whole, which is shorter than its diff:
```python
import functools

import jax
import jax.numpy as jnp
from jax import lax
from jax.experimental import pallas as pl
from jax.experimental.pallas import tpu as pltpu
from jax.sharding import PartitionSpec as P


ROWS = 256
TOKS = 128
WIDE = 2
SPAN = WIDE * TOKS + 16
COLS = 256
EXPERTS = 2
VMEM = 66_000_000

BF = jnp.bfloat16
F32 = jnp.float32


def mm(a, b):
    return lax.dot_general(a, b, (((1,), (0,)), ((), ())), preferred_element_type=F32)


def mm_nt(a, b):
    return lax.dot_general(a, b, (((1,), (1,)), ((), ())), preferred_element_type=F32)


def mm_tn(a, b):
    return lax.dot_general(a, b, (((0,), (0,)), ((), ())), preferred_element_type=F32)


def block_of(refs, b, wide=1):
    size = wide * TOKS
    per = refs[0].shape[0] // size
    return refs[b // per], slice((b % per) * size, (b % per + 1) * size)


def tile_rows(k):
    return pl.ds(pl.multiple_of(k * ROWS, ROWS), ROWS)


class Slots:
    def __init__(self, starts_ref, rows_ref, cols_ref, blocks):
        self.starts_ref, self.rows_ref, self.cols_ref, self.blocks = starts_ref, rows_ref, cols_ref, blocks

    def tiles(self, e):
        return (self.starts_ref[e, self.blocks] + ROWS - 1) // ROWS

    def base(self, e, b):
        return pl.multiple_of((self.starts_ref[e, b] // 16) * 16, 16)

    def col(self, b, i, wide=1):
        size = wide * TOKS
        return self.cols_ref[pl.ds(pl.multiple_of(b * size, size), size), i : i + 1]

    def gate(self, e, b, wide=1):
        if isinstance(e, int):
            return self.col(b, EXPERTS + e, wide)
        return jnp.where(e == 0, self.col(b, EXPERTS, wide), self.col(b, EXPERTS + 1, wide))

    def choice(self, e, b, wide=1):
        return self.col(b, 2 * EXPERTS + e, wide)

    def compact(self, e, makers, outs):
        size = WIDE * TOKS
        line = lax.broadcasted_iota(jnp.int32, (size + 16, size), 0).astype(F32)
        for b in range(self.blocks // WIDE):
            base = self.base(e, b * WIDE)
            slot = self.rows_ref[pl.ds(e, 1), b * size : (b + 1) * size] - base.astype(F32)
            hot = jnp.where(slot == line, 1.0, 0.0).astype(BF)
            for make, out in zip(makers, outs):
                rows = mm(hot, make(b)).astype(BF)
                if b == 0:
                    out[pl.ds(base, size + 16), :] = rows
                else:
                    out[pl.ds(base, 16), :] += rows[:16]
                    out[pl.ds(base + 16, size), :] = rows[16:]
        end = self.base(e, self.blocks - WIDE) + size + 16
        for out in outs:
            out[pl.ds(end, ROWS), :] = jnp.zeros((ROWS, out.shape[1]), BF)

    def spread(self, e, b, ref, wide=1):
        size = wide * TOKS
        base = self.base(e, b * wide)
        line = lax.broadcasted_iota(jnp.int32, (size, size + 16), 1).astype(F32)
        hot = jnp.where(self.col(b, e, wide) - base.astype(F32) == line, 1.0, 0.0).astype(BF)
        return mm(hot, ref[pl.ds(base, size + 16), :])

    def zero_after(self, e, ref):
        end = pl.multiple_of(self.tiles(e) * ROWS, ROWS)
        ref[pl.ds(end, SPAN), :] = jnp.zeros((SPAN, ref.shape[1]), BF)


def routing_kernel(t0, t1, t2, t3, *refs):
    tables = (t0, t1, t2, t3)
    full_a, full_b, halves = refs[0:3], refs[3:6], (refs[6:9], refs[9:12])
    tok = t0.shape[1]
    blocks = len(tables) * tok // TOKS
    half = blocks // 2
    first = (lax.axis_index("ep") * EXPERTS).astype(F32)
    line = lax.broadcasted_iota(jnp.int32, (8, TOKS), 0)
    target = first + (line % EXPERTS).astype(F32)
    lane = lax.broadcasted_iota(jnp.int32, (8, 128), 1)
    upto = (lax.broadcasted_iota(jnp.int32, (TOKS, TOKS), 0) <= lax.broadcasted_iota(jnp.int32, (TOKS, TOKS), 1)).astype(F32).astype(BF)
    seen = jnp.zeros((8, 1), F32)
    before = jnp.zeros((8, 1), F32)
    starts = jnp.zeros((8, 128), F32)
    later = jnp.zeros((8, 128), F32)
    for b in range(blocks):
        at = b * TOKS
        table = tables[at // tok][:, at % tok : at % tok + TOKS]
        if b == half:
            before = seen

        def both(i, other):
            return jnp.where(line < EXPERTS, table[i : i + 1], jnp.where(line < 2 * EXPERTS, table[i + 2 : i + 3], other))

        hit0 = both(0, -1.0) == target
        hit1 = both(1, -1.0) == target
        mask = jnp.where(hit0 | hit1, 1.0, 0.0)
        count = mm(mask.astype(BF), upto)
        slot = jnp.where(mask > 0.0, seen + count - 1.0, -1.0)
        part_slot = jnp.where(mask > 0.0, seen - before + count - 1.0, -1.0)
        gate = jnp.where(hit0, both(4, 0.0), 0.0) + jnp.where(hit1, both(5, 0.0), 0.0)
        choice = jnp.where(hit1, 1.0, 0.0)
        starts = jnp.where(lane == b, seen, starts)
        if b >= half:
            later = jnp.where(lane == b - half, seen - before, later)

        def put(outs, layer, here, slots):
            part = slice(layer * EXPERTS, (layer + 1) * EXPERTS)
            outs[1][:, here : here + TOKS] = slots[part]
            stack = jnp.concatenate([slots[part], gate[part], choice[part], choice[part]], axis=0)
            outs[2][here : here + TOKS, :] = stack.T

        put(full_a, 0, at, slot)
        put(full_b, 1, at, slot)
        put(halves[b // half], 0, at % (half * TOKS), part_slot)
        seen = seen + count[:, TOKS - 1 :]
    starts = jnp.where(lane == blocks, seen, starts).astype(jnp.int32)
    later = jnp.where(lane == half, seen - before, later).astype(jnp.int32)
    full_a[0][...] = starts[:EXPERTS]
    full_b[0][...] = starts[EXPERTS : 2 * EXPERTS]
    halves[0][0][...] = starts[:EXPERTS]
    halves[1][0][...] = later[:EXPERTS]


def weight_copies(hbm, vmem, sems, e):
    return [pltpu.make_async_copy(h.at[e], v.at[e], sems.at[e, i]) for i, (h, v) in enumerate(zip(hbm, vmem))]


def forward_kernel(n, starts_ref, *refs):
    xs, (rows_ref, cols_ref, w1_hbm, w3_hbm, w2_hbm), ys = refs[:n], refs[n : n + 5], refs[n + 5 : 2 * n + 5]
    w1, w3, w2, u_all, o_all, h_ref, y_buf, w_sems, y_sems = refs[2 * n + 5 :]
    blocks = rows_ref.shape[1] // TOKS
    width = w1.shape[2]
    slots = Slots(starts_ref, rows_ref, cols_ref, blocks)
    for e in range(EXPERTS):
        for copy in weight_copies((w1_hbm, w3_hbm, w2_hbm), (w1, w3, w2), w_sems, e):
            copy.start()

    def tokens_of(b):
        ref, toks = block_of(xs, b, WIDE)
        return ref[toks, :]

    def gather_rows(e, carry):
        slots.compact(e, (tokens_of,), (u_all.at[e],))
        return carry

    lax.fori_loop(0, EXPERTS, gather_rows, 0)

    def expert(e, carry):
        for copy in weight_copies((w1_hbm, w3_hbm, w2_hbm), (w1, w3, w2), w_sems, e):
            copy.wait()

        def tile(k, inner):
            u = u_all[e, tile_rows(k), :]
            for c in range(0, width, COLS):
                cols = slice(c, c + COLS)
                a = mm(u, w1[e, :, cols])
                b = mm(u, w3[e, :, cols])
                h_ref[:, cols] = (a * jax.nn.sigmoid(a) * b).astype(BF)
            o_all[e, tile_rows(k), :] = mm(h_ref[...], w2[e]).astype(BF)
            return inner

        return lax.fori_loop(0, slots.tiles(e), tile, carry)

    lax.fori_loop(0, EXPERTS, expert, 0)
    for e in range(EXPERTS):
        slots.zero_after(e, o_all.at[e])
    copies = []
    each = ys[0].shape[0] // TOKS
    for i, ref in enumerate(ys):

        def blocks_of(half, carry):
            for step in range(each // 2):
                j = half * (each // 2) + step
                b = i * each + j
                toks = pl.ds(pl.multiple_of(j * TOKS, TOKS), TOKS)
                y_buf[i, toks, :] = sum(slots.gate(e, b) * slots.spread(e, b, o_all.at[e]) for e in range(EXPERTS))
            return carry

        lax.fori_loop(0, 2, blocks_of, 0)
        copies.append(pltpu.make_async_copy(y_buf.at[i], ref, y_sems.at[i]))
        copies[-1].start()
    for copy in copies:
        copy.wait()


def dx_kernel(starts_ref, x0, x1, x2, x3, g0, g1, g2, g3, rows_ref, cols_ref, w1_hbm, w3_hbm, w2_hbm,
              dx0, dx1, dx2, dx3, kept_hbm, w1, w3, w2, u_all, q_all, od_all, kept, dx_buf, w_sems, k_sems, dx_sems):
    xs, gs, dxs = (x0, x1, x2, x3), (g0, g1, g2, g3), (dx0, dx1, dx2, dx3)
    tok = x0.shape[0]
    blocks = rows_ref.shape[1] // TOKS
    dim, width = w1.shape[1:]
    slots = Slots(starts_ref, rows_ref, cols_ref, blocks)
    for e in range(EXPERTS):
        for copy in weight_copies((w1_hbm, w3_hbm, w2_hbm), (w1, w3, w2), w_sems, e):
            copy.start()

    def tokens_of(b):
        ref, toks = block_of(xs, b, WIDE)
        return ref[toks, :]

    def gather_rows(e, carry):
        def scaled_of(b):
            ref, toks = block_of(gs, b, WIDE)
            return (slots.gate(e, b, WIDE) * ref[toks, :].astype(F32)).astype(BF)

        slots.compact(e, (tokens_of, scaled_of), (u_all.at[e], q_all.at[e]))
        return carry

    lax.fori_loop(0, EXPERTS, gather_rows, 0)

    def copy_out(e, k):
        return pltpu.make_async_copy(kept.at[lax.rem(k, 2)], kept_hbm.at[e, tile_rows(k), :], k_sems.at[lax.rem(k, 2)])

    def expert(e, carry):
        for copy in weight_copies((w1_hbm, w3_hbm, w2_hbm), (w1, w3, w2), w_sems, e):
            copy.wait()
        count = slots.tiles(e)

        def tile(k, inner):
            slot = lax.rem(k, 2)

            @pl.when(k >= 2)
            def _():
                copy_out(e, k - 2).wait()

            u = u_all[e, tile_rows(k), :]
            q = q_all[e, tile_rows(k), :]
            for c in range(0, width, COLS):
                cols = slice(c, c + COLS)
                a = mm(u, w1[e, :, cols])
                b = mm(u, w3[e, :, cols])
                dh = mm_nt(q, w2[e, cols, :])
                s = jax.nn.sigmoid(a)
                act = a * s
                kept[slot, :, c : c + COLS] = (act * b).astype(BF)
                kept[slot, :, width + c : width + c + COLS] = (dh * b * s * (1.0 + a * (1.0 - s))).astype(BF)
                kept[slot, :, 2 * width + c : 2 * width + c + COLS] = (dh * act).astype(BF)
            kept[slot, :, 3 * width : 3 * width + dim] = u
            kept[slot, :, 3 * width + dim :] = q
            od_all[e, tile_rows(k), :dim] = mm(kept[slot, :, :width], w2[e]).astype(BF)
            du = mm_nt(kept[slot, :, width : 2 * width], w1[e]) + mm_nt(kept[slot, :, 2 * width : 3 * width], w3[e])
            od_all[e, tile_rows(k), dim:] = du.astype(BF)
            copy_out(e, k).start()
            return inner

        lax.fori_loop(0, count, tile, 0)

        @pl.when(count >= 2)
        def _():
            copy_out(e, count - 2).wait()

        @pl.when(count >= 1)
        def _():
            copy_out(e, count - 1).wait()

        return carry

    lax.fori_loop(0, EXPERTS, expert, 0)
    for e in range(EXPERTS):
        slots.zero_after(e, od_all.at[e])
    copies = []
    size = WIDE * TOKS
    each = tok // size
    lane = lax.broadcasted_iota(jnp.int32, (size, 8), 1).astype(F32)
    for i, ref in enumerate(dxs):

        for j in range(each):
            b = i * each + j
            toks = slice(j * size, (j + 1) * size)
            dy = gs[i][toks, :].astype(F32)
            dx = jnp.zeros((size, dim), F32)
            dg = jnp.zeros((size, 8), F32)
            for e in range(EXPERTS):
                od = slots.spread(e, b, od_all.at[e], WIDE)
                dx += od[:, dim:]
                dg += jnp.where(lane == slots.choice(e, b, WIDE), jnp.sum(dy * od[:, :dim], axis=1, keepdims=True), 0.0)
            dx_buf[i, toks, :] = dx
            dx_buf[i, tok : tok + 8, toks] = dg.T
        copies.append(pltpu.make_async_copy(dx_buf.at[i], ref, dx_sems.at[i]))
        copies[-1].start()
    for copy in copies:
        copy.wait()


def dw_kernel(starts_ref, kept_hbm, dw1_hbm, dw3_hbm, dw2_hbm, kept, dw1, dw3, dw2, k_sems, o_sems):
    dim, width = dw1.shape[1:]
    slots = Slots(starts_ref, None, None, kept_hbm.shape[1] // TOKS)

    def copy_in(e, k, slot):
        rows = pl.ds(pl.multiple_of(k * 2 * ROWS, 2 * ROWS), 2 * ROWS)
        return pltpu.make_async_copy(kept_hbm.at[e, rows, :], kept.at[slot], k_sems.at[slot])

    def copy_out(e, i):
        return pltpu.make_async_copy((dw1, dw3, dw2)[i].at[e], (dw1_hbm, dw3_hbm, dw2_hbm)[i].at[e], o_sems.at[e, i])

    first_tiles = (slots.tiles(0) + 1) // 2
    count = first_tiles + (slots.tiles(1) + 1) // 2

    def where(g):
        e = (g >= first_tiles).astype(jnp.int32)
        return e, g - e * first_tiles

    copy_in(*where(0), 0).start()

    def tile(g, carry):
        slot = lax.rem(g, 2)
        e, k = where(g)
        copy_in(e, k, slot).wait()

        @pl.when(g + 1 < count)
        def _():
            copy_in(*where(g + 1), 1 - slot).start()

        @pl.when(2 * k + 1 == slots.tiles(e))
        def _():
            kept[slot, ROWS:, :] = jnp.zeros((ROWS, kept.shape[2]), BF)

        u = kept[slot, :, 3 * width : 3 * width + dim]
        q = kept[slot, :, 3 * width + dim :]
        fresh = k == 0
        last = (g == first_tiles - 1) | (g == count - 1)

        def put(ref, index, part):
            ref[index] = jnp.where(fresh, part, ref[index] + part)

        def leave(i):
            pl.when(last)(lambda: copy_out(e, i).start())

        for c in range(0, width, COLS):
            put(dw1, (e, slice(None), slice(c, c + COLS)), mm_tn(u, kept[slot, :, width + c : width + c + COLS]))
        leave(0)
        for c in range(0, width, COLS):
            put(dw3, (e, slice(None), slice(c, c + COLS)), mm_tn(u, kept[slot, :, 2 * width + c : 2 * width + c + COLS]))
        leave(1)
        for c in range(0, width, COLS):
            put(dw2, (e, slice(c, c + COLS), slice(None)), mm_tn(kept[slot, :, c : c + COLS], q))
        leave(2)
        return carry

    lax.fori_loop(0, count, tile, 0)
    for e in range(EXPERTS):
        for i in range(3):
            copy_out(e, i).wait()


IN_VMEM = pl.BlockSpec(memory_space=pltpu.VMEM)
IN_SMEM = pl.BlockSpec(memory_space=pltpu.SMEM)
IN_HBM = pl.BlockSpec(memory_space=pl.ANY)


def call(kernel, operands, in_specs, outs, out_specs, scratch, flops):
    return pl.pallas_call(
        kernel,
        in_specs=in_specs,
        out_specs=out_specs,
        out_shape=outs,
        scratch_shapes=scratch,
        compiler_params=pltpu.CompilerParams(vmem_limit_bytes=VMEM),
        cost_estimate=pl.CostEstimate(flops=flops, bytes_accessed=40_000_000, transcendentals=0),
    )(*operands)


def run_routing(tables):
    tokens = tables[0].shape[1] * len(tables)
    outs = []
    for size in (tokens, tokens, tokens // 2, tokens // 2):
        outs.append(jax.ShapeDtypeStruct((EXPERTS, 128), jnp.int32))
        outs.append(jax.ShapeDtypeStruct((EXPERTS, size), F32))
        outs.append(jax.ShapeDtypeStruct((size, 8), F32))
    maps = call(routing_kernel, tables, [IN_VMEM] * 4, outs, [IN_VMEM] * 12, [], 10_000_000)
    return maps[0:3], maps[3:6], maps[6:9], maps[9:12]


def weight_scratch(w1, w2):
    return [pltpu.VMEM(w1.shape, BF), pltpu.VMEM(w1.shape, BF), pltpu.VMEM(w2.shape, BF)]


def run_forward(xs, maps, w1, w3, w2):
    tok, dim = xs[0].shape
    tokens = tok * len(xs)
    width = w1.shape[2]
    most = tokens + SPAN + ROWS
    return call(
        functools.partial(forward_kernel, len(xs)), (maps[0], *xs, maps[1], maps[2], w1, w3, w2),
        [IN_SMEM] + [IN_VMEM] * (len(xs) + 2) + [IN_HBM] * 3,
        [jax.ShapeDtypeStruct((tok, dim), F32)] * len(xs),
        [IN_HBM] * len(xs),
        weight_scratch(w1, w2)
        + [pltpu.VMEM((EXPERTS, most, dim), BF)] * 2
        + [pltpu.VMEM((ROWS, width), BF), pltpu.VMEM((len(xs), tok, dim), F32)]
        + [pltpu.SemaphoreType.DMA((EXPERTS, 3)), pltpu.SemaphoreType.DMA((len(xs),))],
        2 * 3 * tokens * dim * width,
    )


def run_dx(xs, gs, maps, w1, w3, w2):
    tok, dim = xs[0].shape
    tokens = tok * len(xs)
    width = w1.shape[2]
    most = tokens + SPAN + ROWS
    kept = 3 * width + 2 * dim
    out = call(
        dx_kernel, (maps[0], *xs, *gs, maps[1], maps[2], w1, w3, w2),
        [IN_SMEM] + [IN_VMEM] * 10 + [IN_HBM] * 3,
        [jax.ShapeDtypeStruct((tok + 8, dim), F32)] * 4 + [jax.ShapeDtypeStruct((EXPERTS, tokens, kept), BF)],
        [IN_HBM] * 5,
        weight_scratch(w1, w2)
        + [pltpu.VMEM((EXPERTS, most, dim), BF)] * 2
        + [pltpu.VMEM((EXPERTS, most, 2 * dim), BF), pltpu.VMEM((2, ROWS, kept), BF), pltpu.VMEM((4, tok + 8, dim), F32)]
        + [pltpu.SemaphoreType.DMA((EXPERTS, 3)), pltpu.SemaphoreType.DMA((2,)), pltpu.SemaphoreType.DMA((4,))],
        2 * 6 * tokens * dim * width,
    )
    return out[:4], out[4]


def run_dw(kept, maps, shape1, shape2):
    tokens = kept.shape[1]
    return call(
        dw_kernel, (maps[0], kept),
        [IN_SMEM, IN_HBM],
        [jax.ShapeDtypeStruct(shape1, F32), jax.ShapeDtypeStruct(shape1, F32), jax.ShapeDtypeStruct(shape2, F32)],
        [IN_HBM] * 3,
        [pltpu.VMEM((2, 2 * ROWS, kept.shape[2]), BF), pltpu.VMEM(shape1, F32), pltpu.VMEM(shape1, F32), pltpu.VMEM(shape2, F32)]
        + [pltpu.SemaphoreType.DMA((2,)), pltpu.SemaphoreType.DMA((EXPERTS, 3))],
        2 * 3 * tokens * shape1[1] * shape1[2],
    )


def solution(mesh):
    tok_spec = P(("dp", "ep"))
    w_spec = P("ep")
    across = [(0, 2), (2, 0), (1, 3), (3, 1)]
    beside = [(0, 1), (1, 0), (2, 3), (3, 2)]
    cross = [(0, 3), (3, 0), (1, 2), (2, 1)]

    def permute(v, pairs):
        return lax.ppermute(v, "ep", pairs)

    def gather(own):
        other = permute(own, across)
        return other, permute(other, beside), own, permute(own, beside)

    def gather_direct(own):
        return permute(own, across), permute(own, cross), own, permute(own, beside)

    def combine(parts):
        other, diagonal, own, mate = parts
        theirs = other + permute(diagonal, beside)
        return own + permute(mate, beside) + permute(theirs, across)

    def device_program(x_in, idx_a, idx_b, gate_a, gate_b, dy_out, w1_a, w3_a, w2_a, w1_b, w3_b, w2_b):
        tok, top_k = idx_a.shape
        own_map = jnp.concatenate([idx_a.astype(F32), idx_b.astype(F32), gate_a, gate_b], axis=1).T
        maps_a, maps_b, maps_far, maps_near = run_routing(gather_direct(own_map))

        def add(base, total):
            return (base.astype(F32) + total[:tok]).astype(BF)

        def dgate_of(total):
            return total[tok : tok + top_k].T

        x_all = gather(x_in)
        dy_all = gather(dy_out)
        far_parts = run_forward(x_all[:2], maps_far, w1_a, w3_a, w2_a)
        near_parts = run_forward(x_all[2:], maps_near, w1_a, w3_a, w2_a)
        x_mid = add(x_in, combine((*far_parts, *near_parts)))
        mid_all = gather(x_mid)
        x_again, mid_other = lax.optimization_barrier((x_in, mid_all[0]))
        mid_all = (mid_other, *mid_all[1:])
        again_all = gather_direct(x_again)
        dx_parts, kept_b = run_dx(mid_all, dy_all, maps_b, w1_b, w3_b, w2_b)
        total = combine(dx_parts)
        dx_mid, dgate_b = add(dy_out, total), dgate_of(total)
        dmid_all = gather_direct(dx_mid)
        x_out = add(x_mid, combine(run_forward(mid_all, maps_b, w1_b, w3_b, w2_b)))
        grads_b = run_dw(kept_b, maps_b, w1_b.shape, w2_b.shape)
        dx_parts, kept_a = run_dx(again_all, dmid_all, maps_a, w1_a, w3_a, w2_a)
        total = combine(dx_parts)
        dx_in, dgate_a = add(dx_mid, total), dgate_of(total)
        grads_a = run_dw(kept_a, maps_a, w1_a.shape, w2_a.shape)
        return (x_out, dx_in, *grads_a, *grads_b, dgate_a, dgate_b)


    return jax.shard_map(device_program, mesh=mesh, in_specs=(tok_spec,) * 6 + (w_spec,) * 6, out_specs=(tok_spec,) * 10, check_vma=False)
```

time: 359 us -> 334 us (0.930); the launches traced: 354 us -> 334 us
  waiting for transfers between devices: 120 us -> 109 us
  Pallas kernels: 121 us -> 115 us
    ppermute x30, waiting for transfers between devices: 120 us -> 109 us  [permute(): return lax.ppermute(v, 'ep', pairs)]
    pallas_call x7 -> x8, Pallas kernels: 121 us -> 115 us  [call(): pl.pallas_call(kernel, in_specs=in_specs, out_specs=out_specs, out_shape=...]
  transfers between devices with their start and end apart: 30 -> 30, of which waited for: 14 -> 13; matrix products, arithmetic and copies ran while one was open for 5% -> 5% of each run, Pallas kernels for 22% -> 27%
where the time goes in v3:
time: 334 us
  Pallas kernels  115 us (34%)
  waiting for transfers between devices  109 us (33%)
  starting transfers between devices  83.7 us (25%)
  other arithmetic  19.4 us (6%)
  local copies, waits for them, and re-layouts  4.9 us (1%)
    pallas_call x8, Pallas kernels, call(): pl.pallas_call(kernel, in_specs=in_specs, out_specs=out_specs, out_shape=...  115 us
    ppermute x30, waiting for transfers between devices, permute(): return lax.ppermute(v, 'ep', pairs)  109 us
    ppermute x30, starting transfers between devices, permute(): return lax.ppermute(v, 'ep', pairs)  83.7 us
    add x4, other arithmetic, combine(): theirs = other + permute(diagonal, beside)  7.97 us
  transfers between devices with their start and end apart: 30, of which 13 were waited for; matrix products, arithmetic and copies ran while one was open for 5% of the time, Pallas kernels for 27%

profile of v3, /device:TPU:0, one launch (start us, length us, event | category | flops | bytes accessed | tf_op | source)
XLA Modules:
  0.0 333.8 jit_solution(13164732682127233845)
XLA Ops:
  0.6 3.3 collective-permute-start.5
  4.0 12.1 %collective-permute-done.5.refs_0_ = bf16[512,512]{1,0:T(8,128)(2,1)S(1)} collective-permute-done((bf16[512,512]{1,0:T(8,128)(2,1)}, bf16[512,512]{1,0:T(8,128)(2,1)S(1)}, u32[]{:S(2)}, u32[]{:S(2)}) %collective-permute-start.5) | collective-permute-done | bytes 524320 | tf_op jit(solution)/shard_map/ppermute | solution.py:464
  21.9 1.9 collective-permute-done.t0
  24.5 3.2 shard_map.195
  27.8 9.8 %shard_map.197 = (f32[512,512]{1,0:T(8,128)}, f32[512,512]{1,0:T(8,128)}) custom-call(s32[2,128]{1,0:T(2,128)} %get-tuple-element.53.starts_ref, bf16[512,512]{1,0:T(8,128)(2,1)} %copy-done.20, bf16[512,512]{1,0:T(8,128)(2,1)} %collective-permute-done.6.refs_1_, f32[2,1024]{1,0:T(2,128)} %get-tuple-element.54.refs_2_, f32[1024,8]{1,0:T(8,128)} %get-tuple-element.55.refs_3_, ...), custom_call_target="tpu_custom_call" | custom-call | flops 5637144576 | bytes 40000000 | tf_op jit(solution)/shard_map/pallas_call | solution.py:379
  37.6 9.8 %shard_map.196 = (f32[512,512]{1,0:T(8,128)}, f32[512,512]{1,0:T(8,128)}) custom-call(s32[2,128]{1,0:T(2,128)} %get-tuple-element.48.starts_ref, bf16[512,512]{1,0:T(8,128)(2,1)} %x2, bf16[512,512]{1,0:T(8,128)(2,1)} %collective-permute-done.3.refs_1_, f32[2,1024]{1,0:T(2,128)} %get-tuple-element.49.refs_2_, f32[1024,8]{1,0:T(8,128)} %get-tuple-element.50.refs_3_, ...), custom_call_target="tpu_custom_call" | custom-call | flops 5637144576 | bytes 40000000 | tf_op jit(solution)/shard_map/pallas_call | solution.py:379
  47.9 1.9 add.49
  49.8 9.5 %collective-permute-start.8 = (f32[512,512]{1,0:T(8,128)S(1)}, f32[512,512]{1,0:T(8,128)S(1)}, u32[]{:S(2)}, u32[]{:S(2)}) collective-permute-start(f32[512,512]{1,0:T(8,128)S(1)} %add.49), channel_id=1, source_target_pairs={{0,2},{2,0},{1,3},{3,1},{4,6},{6,4},{5,7},{7,5}} | collective-permute-start | bytes 3145736 | tf_op jit(solution)/shard_map/ppermute | solution.py:464
  59.3 24.0 %collective-permute-done.8 = f32[512,512]{1,0:T(8,128)S(1)} collective-permute-done((f32[512,512]{1,0:T(8,128)S(1)}, f32[512,512]{1,0:T(8,128)S(1)}, u32[]{:S(2)}, u32[]{:S(2)}) %collective-permute-start.8) | collective-permute-done | bytes 1048608 | tf_op jit(solution)/shard_map/ppermute | solution.py:464
  83.7 2.0 collective-permute-start.9
  85.8 8.7 %collective-permute-done.15.g0 = bf16[512,512]{1,0:T(8,128)(2,1)S(1)} collective-permute-done((bf16[512,512]{1,0:T(8,128)(2,1)S(1)}, bf16[512,512]{1,0:T(8,128)(2,1)S(1)}, u32[]{:S(2)}, u32[]{:S(2)}) %collective-permute-start.15) | collective-permute-done | bytes 524320 | tf_op jit(solution)/shard_map/ppermute | solution.py:464
  95.0 10.5 %collective-permute-done.9.refs_0_.x0 = bf16[512,512]{1,0:T(8,128)(2,1)S(1)} collective-permute-done((bf16[512,512]{1,0:T(8,128)(2,1)S(1)}, bf16[512,512]{1,0:T(8,128)(2,1)S(1)}, u32[]{:S(2)}, u32[]{:S(2)}) %collective-permute-start.9) | collective-permute-done | bytes 524320 | tf_op jit(solution)/shard_map/ppermute | solution.py:464
  108.3 24.6 %shard_map.199 = (f32[520,512]{1,0:T(8,128)}, f32[520,512]{1,0:T(8,128)}, f32[520,512]{1,0:T(8,128)}, f32[520,512]{1,0:T(8,128)}, bf16[2,2048,6400]{2,1,0:T(8,128)(2,1)}) custom-call(s32[2,128]{1,0:T(2,128)} %get-tuple-element.58.starts_ref, bf16[512,512]{1,0:T(8,128)(2,1)} %copy-done.18, bf16[512,512]{1,0:T(8,128)(2,1)} %copy-done.24, ...), custom_call_target="tpu_custom_call" | custom-call | flops 22548578304 | bytes 40000000 | tf_op jit(solution)/shard_map/pallas_call | solution.py:379
  133.4 2.4 collective-permute-done.19
  135.8 2.4 add.57
  138.2 20.4 %collective-permute-start.20 = (f32[520,512]{1,0:T(8,128)}, f32[520,512]{1,0:T(8,128)}, u32[]{:S(2)}, u32[]{:S(2)}) collective-permute-start(f32[520,512]{1,0:T(8,128)} %add.57), channel_id=1, source_target_pairs={{0,2},{2,0},{1,3},{3,1},{4,6},{6,4},{5,7},{7,5}} | collective-permute-start | bytes 3194888 | tf_op jit(solution)/shard_map/ppermute | solution.py:464
  158.6 15.0 %shard_map.198 = (f32[512,512]{1,0:T(8,128)}, f32[512,512]{1,0:T(8,128)}, f32[512,512]{1,0:T(8,128)}, f32[512,512]{1,0:T(8,128)}) custom-call(s32[2,128]{1,0:T(2,128)} %get-tuple-element.58.starts_ref, bf16[512,512]{1,0:T(8,128)(2,1)} %copy-done.18, bf16[512,512]{1,0:T(8,128)(2,1)} %copy-done.24, bf16[512,512]{1,0:T(8,128)(2,1)} %copy-done.3, ...), custom_call_target="tpu_custom_call" | custom-call | flops 11274289152 | bytes 40000000 | tf_op jit(solution)/shard_map/pallas_call | solution.py:379
  174.1 9.3 %collective-permute-start.22 = (bf16[512,512]{1,0:T(8,128)(2,1)S(1)}, bf16[512,512]{1,0:T(8,128)(2,1)S(1)}, u32[]{:S(2)}, u32[]{:S(2)}) collective-permute-start(bf16[512,512]{1,0:T(8,128)(2,1)S(1)} %copy-done.11), channel_id=1, source_target_pairs={{0,3},{3,0},{1,2},{2,1},{4,7},{7,4},{5,6},{6,5}} | collective-permute-start | bytes 1572872 | tf_op jit(solution)/shard_map/ppermute | solution.py:464
  183.7 2.3 add_add_fusion.1
  189.7 6.0 %collective-permute-done.22.x1 = bf16[512,512]{1,0:T(8,128)(2,1)S(1)} collective-permute-done((bf16[512,512]{1,0:T(8,128)(2,1)S(1)}, bf16[512,512]{1,0:T(8,128)(2,1)S(1)}, u32[]{:S(2)}, u32[]{:S(2)}) %collective-permute-start.22) | collective-permute-done | bytes 524320 | tf_op jit(solution)/shard_map/ppermute | solution.py:464
  196.3 11.4 %collective-permute-done.21.x0 = bf16[512,512]{1,0:T(8,128)(2,1)S(1)} collective-permute-done((bf16[512,512]{1,0:T(8,128)(2,1)S(1)}, bf16[512,512]{1,0:T(8,128)(2,1)S(1)}, u32[]{:S(2)}, u32[]{:S(2)}) %collective-permute-start.21) | collective-permute-done | bytes 524320 | tf_op jit(solution)/shard_map/ppermute | solution.py:464
  207.7 1.7 collective-permute-start.14
  209.4 8.7 %collective-permute-done.25.g1 = bf16[512,512]{1,0:T(8,128)(2,1)S(1)} collective-permute-done((bf16[512,512]{1,0:T(8,128)(2,1)S(1)}, bf16[512,512]{1,0:T(8,128)(2,1)S(1)}, u32[]{:S(2)}, u32[]{:S(2)}) %collective-permute-start.25) | collective-permute-done | bytes 524320 | tf_op jit(solution)/shard_map/ppermute | solution.py:464
  218.2 12.0 %collective-permute-done.24.g0 = bf16[512,512]{1,0:T(8,128)(2,1)S(1)} collective-permute-done((bf16[512,512]{1,0:T(8,128)(2,1)S(1)}, bf16[512,512]{1,0:T(8,128)(2,1)S(1)}, u32[]{:S(2)}, u32[]{:S(2)}) %collective-permute-start.24) | collective-permute-done | bytes 524320 | tf_op jit(solution)/shard_map/ppermute | solution.py:464
  231.0 24.9 %shard_map.200 = (f32[520,512]{1,0:T(8,128)}, f32[520,512]{1,0:T(8,128)}, f32[520,512]{1,0:T(8,128)}, f32[520,512]{1,0:T(8,128)}, bf16[2,2048,6400]{2,1,0:T(8,128)(2,1)}) custom-call(s32[2,128]{1,0:T(2,128)} %get-tuple-element.70.starts_ref, bf16[512,512]{1,0:T(8,128)(2,1)} %copy-done.19, bf16[512,512]{1,0:T(8,128)(2,1)} %copy-done.17, bf16[512,512]{1,0:T(8,128)(2,1)} %x2, ...), custom_call_target="tpu_custom_call" | custom-call | flops 22548578304 | bytes 40000000 | tf_op jit(solution)/shard_map/pallas_call | solution.py:379
  255.9 14.2 %shard_map.202 = (f32[2,512,1792]{2,1,0:T(8,128)}, f32[2,512,1792]{2,1,0:T(8,128)}, f32[2,1792,512]{2,1,0:T(8,128)}) custom-call(s32[2,128]{1,0:T(2,128)} %get-tuple-element.58.starts_ref, bf16[2,2048,6400]{2,1,0:T(8,128)(2,1)} %get-tuple-element.82.kept_hbm), custom_call_target="tpu_custom_call" | custom-call | flops 11274289152 | bytes 40000000 | tf_op jit(solution)/shard_map/pallas_call | solution.py:379
  270.2 3.2 add_convert_fusion
  273.8 2.4 add.61
  276.2 29.2 %collective-permute-start.29 = (f32[520,512]{1,0:T(8,128)}, f32[520,512]{1,0:T(8,128)}, u32[]{:S(2)}, u32[]{:S(2)}) collective-permute-start(f32[520,512]{1,0:T(8,128)} %add.61), channel_id=1, source_target_pairs={{0,2},{2,0},{1,3},{3,1},{4,6},{6,4},{5,7},{7,5}} | collective-permute-start | bytes 3194888 | tf_op jit(solution)/shard_map/ppermute | solution.py:464
  306.8 14.0 %shard_map.201 = (f32[2,512,1792]{2,1,0:T(8,128)}, f32[2,512,1792]{2,1,0:T(8,128)}, f32[2,1792,512]{2,1,0:T(8,128)}) custom-call(s32[2,128]{1,0:T(2,128)} %get-tuple-element.70.starts_ref, bf16[2,2048,6400]{2,1,0:T(8,128)(2,1)} %get-tuple-element.78.kept_hbm), custom_call_target="tpu_custom_call" | custom-call | flops 11274289152 | bytes 40000000 | tf_op jit(solution)/shard_map/pallas_call | solution.py:379
  320.8 9.1 %collective-permute-done.29 = f32[520,512]{1,0:T(8,128)} collective-permute-done((f32[520,512]{1,0:T(8,128)}, f32[520,512]{1,0:T(8,128)}, u32[]{:S(2)}, u32[]{:S(2)}) %collective-permute-start.29) | collective-permute-done | bytes 1064992 | tf_op jit(solution)/shard_map/ppermute | solution.py:464
  330.0 2.3 add_add_fusion
  (109 shorter events, 20.4 us)
Async XLA Ops:
  0.6 15.5 %collective-permute-start.5 = (bf16[512,512]{1,0:T(8,128)(2,1)}, bf16[512,512]{1,0:T(8,128)(2,1)S(1)}, u32[]{:S(2)}, u32[]{:S(2)}) collective-permute-start(bf16[512,512]{1,0:T(8,128)(2,1)} %x2), channel_id=1, source_target_pairs={{0,2},{2,0},{1,3},{3,1},{4,6},{6,4},{5,7},{7,5}} | collective-permute-start | bytes 1572872 | tf_op jit(solution)/shard_map/ppermute | solution.py:464
  16.1 11.6 %collective-permute-start.6 = (bf16[512,512]{1,0:T(8,128)(2,1)S(1)}, bf16[512,512]{1,0:T(8,128)(2,1)}, u32[]{:S(2)}, u32[]{:S(2)}) collective-permute-start(bf16[512,512]{1,0:T(8,128)(2,1)S(1)} %collective-permute-done.5.refs_0_), channel_id=1, source_target_pairs={{0,1},{1,0},{2,3},{3,2},{4,5},{5,4},{6,7},{7,6}} | collective-permute-start | bytes 1572872 | tf_op jit(solution)/shard_map/ppermute | solution.py:464
  18.2 2.4 collective-permute-start.2
  18.8 3.2 collective-permute-start.1
  20.1 3.7 %collective-permute-start = (f32[8,512]{1,0:T(8,128)S(1)}, f32[8,512]{1,0:T(8,128)S(1)}, u32[]{:S(2)}, u32[]{:S(2)}) collective-permute-start(f32[8,512]{1,0:T(8,128)S(1)} %maximum_bitcast_fusion.t2), channel_id=1, source_target_pairs={{0,2},{2,0},{1,3},{3,1},{4,6},{6,4},{5,7},{7,5}} | collective-permute-start | bytes 49160 | tf_op jit(solution)/shard_map/ppermute | solution.py:464
  20.5 17.1 %collective-permute-start.3 = (bf16[512,512]{1,0:T(8,128)(2,1)}, bf16[512,512]{1,0:T(8,128)(2,1)}, u32[]{:S(2)}, u32[]{:S(2)}) collective-permute-start(bf16[512,512]{1,0:T(8,128)(2,1)} %x2), channel_id=1, source_target_pairs={{0,1},{1,0},{2,3},{3,2},{4,5},{5,4},{6,7},{7,6}} | collective-permute-start | bytes 1572872 | tf_op jit(solution)/shard_map/ppermute | solution.py:464
  37.5 10.3 %collective-permute-start.7 = (f32[512,512]{1,0:T(8,128)}, f32[512,512]{1,0:T(8,128)}, u32[]{:S(2)}, u32[]{:S(2)}) collective-permute-start(f32[512,512]{1,0:T(8,128)} %get-tuple-element.57), channel_id=1, source_target_pairs={{0,1},{1,0},{2,3},{3,2},{4,5},{5,4},{6,7},{7,6}} | collective-permute-start | bytes 3145736 | tf_op jit(solution)/shard_map/ppermute | solution.py:464
  47.3 12.0 %collective-permute-start.4 = (f32[512,512]{1,0:T(8,128)}, f32[512,512]{1,0:T(8,128)S(1)}, u32[]{:S(2)}, u32[]{:S(2)}) collective-permute-start(f32[512,512]{1,0:T(8,128)} %get-tuple-element.52), channel_id=1, source_target_pairs={{0,1},{1,0},{2,3},{3,2},{4,5},{5,4},{6,7},{7,6}} | collective-permute-start | bytes 3145736 | tf_op jit(solution)/shard_map/ppermute | solution.py:464
  47.8 35.5 %copy-start.7 = (f32[512,512]{1,0:T(8,128)S(1)}, f32[512,512]{1,0:T(8,128)}, u32[]{:S(2)}) copy-start(f32[512,512]{1,0:T(8,128)} %get-tuple-element.51) | copy-start | bytes 3145732
  47.8 35.5 %copy-start.10 = (bf16[512,512]{1,0:T(8,128)(2,1)S(1)}, bf16[512,512]{1,0:T(8,128)(2,1)}, u32[]{:S(2)}) copy-start(bf16[512,512]{1,0:T(8,128)(2,1)} %x2) | copy-start | bytes 1572868
  49.8 33.5 %collective-permute-start.8 = (f32[512,512]{1,0:T(8,128)S(1)}, f32[512,512]{1,0:T(8,128)S(1)}, u32[]{:S(2)}, u32[]{:S(2)}) collective-permute-start(f32[512,512]{1,0:T(8,128)S(1)} %add.49), channel_id=1, source_target_pairs={{0,2},{2,0},{1,3},{3,1},{4,6},{6,4},{5,7},{7,5}} | collective-permute-start | bytes 3145736 | tf_op jit(solution)/shard_map/ppermute | solution.py:464
  59.3 35.2 %collective-permute-start.15 = (bf16[512,512]{1,0:T(8,128)(2,1)S(1)}, bf16[512,512]{1,0:T(8,128)(2,1)S(1)}, u32[]{:S(2)}, u32[]{:S(2)}) collective-permute-start(bf16[512,512]{1,0:T(8,128)(2,1)S(1)} %copy-done.8), channel_id=1, source_target_pairs={{0,2},{2,0},{1,3},{3,1},{4,6},{6,4},{5,7},{7,5}} | collective-permute-start | bytes 1572872 | tf_op jit(solution)/shard_map/ppermute | solution.py:464
  83.7 21.8 %collective-permute-start.9 = (bf16[512,512]{1,0:T(8,128)(2,1)S(1)}, bf16[512,512]{1,0:T(8,128)(2,1)S(1)}, u32[]{:S(2)}, u32[]{:S(2)}) collective-permute-start(bf16[512,512]{1,0:T(8,128)(2,1)S(1)} %add_convert_fusion.1.refs_2_.x2), channel_id=1, source_target_pairs={{0,2},{2,0},{1,3},{3,1},{4,6},{6,4},{5,7},{7,5}} | collective-permute-start | bytes 1572872 | tf_op jit(solution)/shard_map/ppermute | solution.py:464
  85.8 19.8 %collective-permute-start.17 = (bf16[512,512]{1,0:T(8,128)(2,1)S(1)}, bf16[512,512]{1,0:T(8,128)(2,1)S(1)}, u32[]{:S(2)}, u32[]{:S(2)}) collective-permute-start(bf16[512,512]{1,0:T(8,128)(2,1)S(1)} %copy-done.8), channel_id=1, source_target_pairs={{0,1},{1,0},{2,3},{3,2},{4,5},{5,4},{6,7},{7,6}} | collective-permute-start | bytes 1572872 | tf_op jit(solution)/shard_map/ppermute | solution.py:464
  94.5 11.0 %collective-permute-start.16 = (bf16[512,512]{1,0:T(8,128)(2,1)S(1)}, bf16[512,512]{1,0:T(8,128)(2,1)S(1)}, u32[]{:S(2)}, u32[]{:S(2)}) collective-permute-start(bf16[512,512]{1,0:T(8,128)(2,1)S(1)} %collective-permute-done.15.g0), channel_id=1, source_target_pairs={{0,1},{1,0},{2,3},{3,2},{4,5},{5,4},{6,7},{7,6}} | collective-permute-start | bytes 1572872 | tf_op jit(solution)/shard_map/ppermute | solution.py:464
  94.5 11.1 %collective-permute-start.11 = (bf16[512,512]{1,0:T(8,128)(2,1)S(1)}, bf16[512,512]{1,0:T(8,128)(2,1)S(1)}, u32[]{:S(2)}, u32[]{:S(2)}) collective-permute-start(bf16[512,512]{1,0:T(8,128)(2,1)S(1)} %add_convert_fusion.1.refs_2_.x2), channel_id=1, source_target_pairs={{0,1},{1,0},{2,3},{3,2},{4,5},{5,4},{6,7},{7,6}} | collective-permute-start | bytes 1572872 | tf_op jit(solution)/shard_map/ppermute | solution.py:464
  105.5 1.9 collective-permute-start.10
  132.8 2.9 collective-permute-start.19
  133.0 50.4 %collective-permute-start.18 = (f32[520,512]{1,0:T(8,128)}, f32[520,512]{1,0:T(8,128)}, u32[]{:S(2)}, u32[]{:S(2)}) collective-permute-start(f32[520,512]{1,0:T(8,128)} %get-tuple-element.67), channel_id=1, source_target_pairs={{0,1},{1,0},{2,3},{3,2},{4,5},{5,4},{6,7},{7,6}} | collective-permute-start | bytes 3194888 | tf_op jit(solution)/shard_map/ppermute | solution.py:464
  138.2 45.6 %collective-permute-start.20 = (f32[520,512]{1,0:T(8,128)}, f32[520,512]{1,0:T(8,128)}, u32[]{:S(2)}, u32[]{:S(2)}) collective-permute-start(f32[520,512]{1,0:T(8,128)} %add.57), channel_id=1, source_target_pairs={{0,2},{2,0},{1,3},{3,1},{4,6},{6,4},{5,7},{7,5}} | collective-permute-start | bytes 3194888 | tf_op jit(solution)/shard_map/ppermute | solution.py:464
  173.6 14.5 %collective-permute-start.13 = (f32[512,512]{1,0:T(8,128)}, f32[512,512]{1,0:T(8,128)S(1)}, u32[]{:S(2)}, u32[]{:S(2)}) collective-permute-start(f32[512,512]{1,0:T(8,128)} %get-tuple-element.65), channel_id=1, source_target_pairs={{0,1},{1,0},{2,3},{3,2},{4,5},{5,4},{6,7},{7,6}} | collective-permute-start | bytes 3145736 | tf_op jit(solution)/shard_map/ppermute | solution.py:464
  173.6 12.8 %collective-permute-start.23 = (bf16[512,512]{1,0:T(8,128)(2,1)S(1)}, bf16[512,512]{1,0:T(8,128)(2,1)S(1)}, u32[]{:S(2)}, u32[]{:S(2)}) collective-permute-start(bf16[512,512]{1,0:T(8,128)(2,1)S(1)} %copy-done.11), channel_id=1, source_target_pairs={{0,1},{1,0},{2,3},{3,2},{4,5},{5,4},{6,7},{7,6}} | collective-permute-start | bytes 1572872 | tf_op jit(solution)/shard_map/ppermute | solution.py:464
  174.1 21.6 %collective-permute-start.22 = (bf16[512,512]{1,0:T(8,128)(2,1)S(1)}, bf16[512,512]{1,0:T(8,128)(2,1)S(1)}, u32[]{:S(2)}, u32[]{:S(2)}) collective-permute-start(bf16[512,512]{1,0:T(8,128)(2,1)S(1)} %copy-done.11), channel_id=1, source_target_pairs={{0,3},{3,0},{1,2},{2,1},{4,7},{7,4},{5,6},{6,5}} | collective-permute-start | bytes 1572872 | tf_op jit(solution)/shard_map/ppermute | solution.py:464
  183.4 24.4 %collective-permute-start.21 = (bf16[512,512]{1,0:T(8,128)(2,1)S(1)}, bf16[512,512]{1,0:T(8,128)(2,1)S(1)}, u32[]{:S(2)}, u32[]{:S(2)}) collective-permute-start(bf16[512,512]{1,0:T(8,128)(2,1)S(1)} %copy-done.11), channel_id=1, source_target_pairs={{0,2},{2,0},{1,3},{3,1},{4,6},{6,4},{5,7},{7,5}} | collective-permute-start | bytes 1572872 | tf_op jit(solution)/shard_map/ppermute | solution.py:464
  186.3 23.2 %collective-permute-start.26 = (bf16[512,512]{1,0:T(8,128)(2,1)S(1)}, bf16[512,512]{1,0:T(8,128)(2,1)S(1)}, u32[]{:S(2)}, u32[]{:S(2)}) collective-permute-start(bf16[512,512]{1,0:T(8,128)(2,1)S(1)} %fusion.1.g2), channel_id=1, source_target_pairs={{0,1},{1,0},{2,3},{3,2},{4,5},{5,4},{6,7},{7,6}} | collective-permute-start | bytes 1572872 | tf_op jit(solution)/shard_map/ppermute | solution.py:464
  186.4 31.8 %collective-permute-start.25 = (bf16[512,512]{1,0:T(8,128)(2,1)S(1)}, bf16[512,512]{1,0:T(8,128)(2,1)S(1)}, u32[]{:S(2)}, u32[]{:S(2)}) collective-permute-start(bf16[512,512]{1,0:T(8,128)(2,1)S(1)} %fusion.1.g2), channel_id=1, source_target_pairs={{0,3},{3,0},{1,2},{2,1},{4,7},{7,4},{5,6},{6,5}} | collective-permute-start | bytes 1572872 | tf_op jit(solution)/shard_map/ppermute | solution.py:464
  188.1 42.1 %collective-permute-start.24 = (bf16[512,512]{1,0:T(8,128)(2,1)S(1)}, bf16[512,512]{1,0:T(8,128)(2,1)S(1)}, u32[]{:S(2)}, u32[]{:S(2)}) collective-permute-start(bf16[512,512]{1,0:T(8,128)(2,1)S(1)} %fusion.1.g2), channel_id=1, source_target_pairs={{0,2},{2,0},{1,3},{3,1},{4,6},{6,4},{5,7},{7,5}} | collective-permute-start | bytes 1572872 | tf_op jit(solution)/shard_map/ppermute | solution.py:464
  195.7 74.4 %collective-permute-start.12 = (f32[512,512]{1,0:T(8,128)}, f32[512,512]{1,0:T(8,128)}, u32[]{:S(2)}, u32[]{:S(2)}) collective-permute-start(f32[512,512]{1,0:T(8,128)} %get-tuple-element.63), channel_id=1, source_target_pairs={{0,1},{1,0},{2,3},{3,2},{4,5},{5,4},{6,7},{7,6}} | collective-permute-start | bytes 3145736 | tf_op jit(solution)/shard_map/ppermute | solution.py:464
  207.7 62.4 %collective-permute-start.14 = (f32[512,512]{1,0:T(8,128)}, f32[512,512]{1,0:T(8,128)}, u32[]{:S(2)}, u32[]{:S(2)}) collective-permute-start(f32[512,512]{1,0:T(8,128)} %add.53), channel_id=1, source_target_pairs={{0,2},{2,0},{1,3},{3,1},{4,6},{6,4},{5,7},{7,5}} | collective-permute-start | bytes 3145736 | tf_op jit(solution)/shard_map/ppermute | solution.py:464
  255.9 17.9 %collective-permute-start.28 = (f32[520,512]{1,0:T(8,128)}, f32[520,512]{1,0:T(8,128)}, u32[]{:S(2)}, u32[]{:S(2)}) collective-permute-start(f32[520,512]{1,0:T(8,128)} %get-tuple-element.77), channel_id=1, source_target_pairs={{0,1},{1,0},{2,3},{3,2},{4,5},{5,4},{6,7},{7,6}} | collective-permute-start | bytes 3194888 | tf_op jit(solution)/shard_map/ppermute | solution.py:464
  273.3 47.5 %collective-permute-start.27 = (f32[520,512]{1,0:T(8,128)}, f32[520,512]{1,0:T(8,128)}, u32[]{:S(2)}, u32[]{:S(2)}) collective-permute-start(f32[520,512]{1,0:T(8,128)} %get-tuple-element.75), channel_id=1, source_target_pairs={{0,1},{1,0},{2,3},{3,2},{4,5},{5,4},{6,7},{7,6}} | collective-permute-start | bytes 3194888 | tf_op jit(solution)/shard_map/ppermute | solution.py:464
  276.2 53.7 %collective-permute-start.29 = (f32[520,512]{1,0:T(8,128)}, f32[520,512]{1,0:T(8,128)}, u32[]{:S(2)}, u32[]{:S(2)}) collective-permute-start(f32[520,512]{1,0:T(8,128)} %add.61), channel_id=1, source_target_pairs={{0,2},{2,0},{1,3},{3,1},{4,6},{6,4},{5,7},{7,5}} | collective-permute-start | bytes 3194888 | tf_op jit(solution)/shard_map/ppermute | solution.py:464
  (27 other events, 239.7 us)
